TPU v7x, 128 devices: a whole 4x4x4 slice. The times are simulated.
128 devices in a mesh: fsdp: 128 (over z, y, x, core).
Axes of the slice: x: 4, y: 4, z: 4, core: 2. Of those that a mesh axis runs over, the one named last changes fastest.
Arguments:
- x_saved: bfloat16 [2, 128, 384, 1280], P(None, 'fsdp')
- grad_out: bfloat16 [128, 384, 1280], P('fsdp')
- x_next: bfloat16 [128, 384, 1280], P('fsdp')
- w_up: bfloat16 [2, 1280, 5120], replicated
- w_down: bfloat16 [2, 5120, 1280], replicated
- gacc_up: float32 [2, 1280, 5120], P(None, 'fsdp')
- gacc_down: float32 [2, 5120, 1280], P(None, 'fsdp')
- master_up: float32 [2, 1280, 5120], P(None, 'fsdp')
- master_down: float32 [2, 5120, 1280], P(None, 'fsdp')
- mom1_up: float32 [2, 1280, 5120], P(None, 'fsdp')
- mom1_down: float32 [2, 5120, 1280], P(None, 'fsdp')
- mom2_up: float32 [2, 1280, 5120], P(None, 'fsdp')
- mom2_down: float32 [2, 5120, 1280], P(None, 'fsdp')
Outputs:
- output 1: bfloat16 [128, 384, 1280], P('fsdp')
- output 2: float32 [2, 1280, 5120], P(None, 'fsdp')
- output 3: float32 [2, 5120, 1280], P(None, 'fsdp')
- output 4: float32 [2, 1280, 5120], P(None, 'fsdp')
- output 5: float32 [2, 5120, 1280], P(None, 'fsdp')
- output 6: float32 [2, 1280, 5120], P(None, 'fsdp')
- output 7: float32 [2, 5120, 1280], P(None, 'fsdp')
All inputs are finite; a program needn't handle non-finite values.
Results may differ from a plain program's by a relative error of at most 0.00841215.
Values are sent between devices in bfloat16 or wider.
A program may use at most 1 GiB of HBM per device.

v0:
```python
import math
import jax
import jax.numpy as jnp
from jax import lax
from jax.sharding import PartitionSpec as P

LEARN_RATE = 0.001
BETA_ONE = 0.9
BETA_TWO = 0.95
ADAM_EPS = 1e-8
WEIGHT_DECAY = 0.1
ADAM_STEP = 3
MICRO_STEPS = 2


def gelu_fn(pre_act):
    return jax.nn.gelu(pre_act, approximate=True)


def adamw_update(master_old, mom_one, mom_two, grad_clip):
    mom_one_new = BETA_ONE * mom_one + (1.0 - BETA_ONE) * grad_clip
    mom_two_new = BETA_TWO * mom_two + (1.0 - BETA_TWO) * grad_clip * grad_clip
    first_hat = mom_one_new / (1.0 - BETA_ONE ** ADAM_STEP)
    second_hat = mom_two_new / (1.0 - BETA_TWO ** ADAM_STEP)
    master_new = master_old - LEARN_RATE * (first_hat / (jnp.sqrt(second_hat) + ADAM_EPS) + WEIGHT_DECAY * master_old)
    return master_new, mom_one_new, mom_two_new


def reduce_rows(part_grad, n_dev):
    received = lax.all_to_all(part_grad, "fsdp", 0, 0, tiled=True)
    return jnp.sum(received.reshape(n_dev, -1, part_grad.shape[1]), axis=0, dtype=jnp.float32)


def backward_update(x_saved, grad_out, w_up, w_down, gacc_up, gacc_down, master_up, master_down, mom1_up, mom1_down, mom2_up, mom2_down, n_dev):
    layers, model_width, ff_width = w_up.shape
    clip_norm = 0.1 * math.sqrt(2 * layers * model_width * ff_width)
    x_tokens = x_saved.reshape(layers, -1, model_width)
    grad_cur = grad_out.reshape(-1, model_width)
    sums_up = []
    sums_down = []
    for layer_idx in range(layers - 1, -1, -1):
        x_in = x_tokens[layer_idx]
        pre_act = jnp.dot(x_in, w_up[layer_idx], preferred_element_type=jnp.float32)
        hidden_act, gelu_vjp = jax.vjp(gelu_fn, pre_act)
        d_act = lax.dot_general(grad_cur, w_down[layer_idx], (((1,), (1,)), ((), ())), preferred_element_type=jnp.float32)
        d_pre = gelu_vjp(d_act)[0].astype(jnp.bfloat16)
        part_down = lax.dot_general(hidden_act.astype(jnp.bfloat16), grad_cur, (((0,), (0,)), ((), ())), preferred_element_type=jnp.float32).astype(jnp.bfloat16)
        part_up = lax.dot_general(x_in, d_pre, (((0,), (0,)), ((), ())), preferred_element_type=jnp.float32).astype(jnp.bfloat16)
        if layer_idx > 0:
            grad_cur = (grad_cur.astype(jnp.float32) + lax.dot_general(d_pre, w_up[layer_idx], (((1,), (1,)), ((), ())), preferred_element_type=jnp.float32)).astype(jnp.bfloat16)
        sums_down.append(reduce_rows(part_down, n_dev))
        sums_up.append(reduce_rows(part_up, n_dev))
    grad_up = (gacc_up + jnp.stack(sums_up[::-1])) / MICRO_STEPS
    grad_down = (gacc_down + jnp.stack(sums_down[::-1])) / MICRO_STEPS
    local_sq = jnp.sum(grad_up * grad_up) + jnp.sum(grad_down * grad_down)
    clip_factor = jnp.minimum(1.0, clip_norm / jnp.sqrt(lax.psum(local_sq, "fsdp")))
    new_up = adamw_update(master_up, mom1_up, mom2_up, grad_up * clip_factor)
    new_down = adamw_update(master_down, mom1_down, mom2_down, grad_down * clip_factor)
    return new_up, new_down


def solution(mesh):
    n_dev = mesh.shape["fsdp"]
    rows_spec = P(None, "fsdp")

    def local_step(x_saved, grad_out, x_next, w_up, w_down, gacc_up, gacc_down, master_up, master_down, mom1_up, mom1_down, mom2_up, mom2_down):
        new_up, new_down = backward_update(x_saved, grad_out, w_up, w_down, gacc_up, gacc_down, master_up, master_down, mom1_up, mom1_down, mom2_up, mom2_down, n_dev)
        up_shard = new_up[0].astype(jnp.bfloat16)
        down_shard = new_down[0].astype(jnp.bfloat16)
        hidden_state = x_next.reshape(-1, x_next.shape[2])
        for layer_idx in range(up_shard.shape[0]):
            w_layer_up = lax.all_gather(up_shard[layer_idx], "fsdp", axis=0, tiled=True)
            w_layer_down = lax.all_gather(down_shard[layer_idx], "fsdp", axis=0, tiled=True)
            pre_act = jnp.dot(hidden_state, w_layer_up, preferred_element_type=jnp.float32)
            hidden_act = gelu_fn(pre_act).astype(jnp.bfloat16)
            hidden_state = (hidden_state.astype(jnp.float32) + jnp.dot(hidden_act, w_layer_down, preferred_element_type=jnp.float32)).astype(jnp.bfloat16)
        return (hidden_state.reshape(x_next.shape), new_up[0], new_down[0], new_up[1], new_down[1], new_up[2], new_down[2])

    return jax.shard_map(local_step, mesh=mesh, in_specs=(rows_spec, P("fsdp"), P("fsdp"), P(), P(), rows_spec, rows_spec, rows_spec, rows_spec, rows_spec, rows_spec, rows_spec, rows_spec), out_specs=(P("fsdp"), rows_spec, rows_spec, rows_spec, rows_spec, rows_spec, rows_spec), check_vma=False)
```

profile of v0, /device:TPU:0, one launch (start us, length us, event | category | flops | bytes accessed | tf_op | source)
XLA Modules:
  0.0 1567.6 jit_solution(13245898006830036815)
XLA Ops:
  7.2 8.6 fusion.18
  15.8 15.9 %fusion.33 = bf16[384,5120]{1,0:T(8,128)(2,1)} fusion(f32[384,5120]{1,0:T(8,128)S(1)} %fusion.18, bf16[2,5120,1280]{2,1,0:T(8,128)(2,1)} %param.17, bf16[1,384,1280]{2,1,0:T(8,128)(2,1)S(1)} %copy-done.6), kind=kOutput, calls=%fused_computation.47 | convolution fusion | flops 5072486400 | bytes 25886720 | tf_op jit(solution)/shard_map/dot_general | solution.py:45
  31.7 12.1 fusion.1
  43.8 24.0 %all_to_all.26 = bf16[128,10,5120]{2,1,0:T(8,128)(2,1)} reshape(bf16[1280,5120]{1,0:T(8,128)(2,1)} %fusion.1) | data formatting | bytes 26214400 | tf_op jit(solution)/shard_map/all_to_all | solution.py:30
  67.8 12.1 all-to-all-start.1
  80.0 12.3 fusion.12
  92.3 9.5 fusion.106
  101.8 19.9 %fusion = bf16[1280,5120]{1,0:T(8,128)(2,1)} fusion(f32[384,5120]{1,0:T(8,128)} %fusion.12, bf16[384,1280]{1,0:T(8,128)(2,1)} %fusion.106, bf16[2,5120,1280]{2,1,0:T(8,128)(2,1)} %param.17, bf16[2,1,384,1280]{3,2,1,0:T(8,128)(2,1)S(1)} %copy-done.5), kind=kOutput, calls=%fused_computation.8 | convolution fusion | flops 10112204800 | bytes 36044800 | tf_op jit(solution)/shard_map/dot_general | solution.py:48
  121.7 24.0 %all_to_all.24 = bf16[128,10,5120]{2,1,0:T(8,128)(2,1)} reshape(bf16[1280,5120]{1,0:T(8,128)(2,1)} %fusion) | data formatting | bytes 26214400 | tf_op jit(solution)/shard_map/all_to_all | solution.py:30
  145.7 238.4 %all-to-all-done.1 = bf16[128,10,5120]{2,1,0:T(8,128)(2,1)} async-done(((bf16[128,10,5120]{2,1,0:T(8,128)(2,1)}), bf16[128,10,5120]{2,1,0:T(8,128)(2,1)}, u32[]{:S(2)}, u32[]{:S(2)}) %all-to-all-start.1) | async-done | bytes 13107232 | tf_op jit(solution)/shard_map/all_to_all | solution.py:30
  384.0 23.5 %all-to-all-start = ((bf16[128,10,5120]{2,1,0:T(8,128)(2,1)}), bf16[128,10,5120]{2,1,0:T(8,128)(2,1)}, u32[]{:S(2)}, u32[]{:S(2)}) async-start(bf16[128,10,5120]{2,1,0:T(8,128)(2,1)} %all_to_all.24), calls=%async_computation | async-start | bytes 41943040 | tf_op jit(solution)/shard_map/all_to_all | solution.py:30
  407.6 15.5 convolution_convert_fusion
  423.1 288.5 %all-to-all-done = bf16[128,10,5120]{2,1,0:T(8,128)(2,1)} async-done(((bf16[128,10,5120]{2,1,0:T(8,128)(2,1)}), bf16[128,10,5120]{2,1,0:T(8,128)(2,1)}, u32[]{:S(2)}, u32[]{:S(2)}) %all-to-all-start) | async-done | bytes 13107232 | tf_op jit(solution)/shard_map/all_to_all | solution.py:30
  711.6 23.3 %all-to-all-start.3 = ((bf16[128,40,1280]{2,1,0:T(8,128)(2,1)}), bf16[128,40,1280]{2,1,0:T(8,128)(2,1)}, u32[]{:S(2)}, u32[]{:S(2)}) async-start(bf16[128,40,1280]{2,1,0:T(8,128)(2,1)} %bitcast.110), calls=%async_computation.3 | async-start | bytes 26214400 | tf_op jit(solution)/shard_map/all_to_all | solution.py:30
  735.0 15.5 convolution_convert_fusion.1
  750.5 159.5 %all-to-all-done.3 = bf16[128,40,1280]{2,1,0:T(8,128)(2,1)} async-done(((bf16[128,40,1280]{2,1,0:T(8,128)(2,1)}), bf16[128,40,1280]{2,1,0:T(8,128)(2,1)}, u32[]{:S(2)}, u32[]{:S(2)}) %all-to-all-start.3) | async-done | bytes 13107232 | tf_op jit(solution)/shard_map/all_to_all | solution.py:30
  910.0 21.5 %all-to-all-start.2 = ((bf16[128,40,1280]{2,1,0:T(8,128)(2,1)}), bf16[128,40,1280]{2,1,0:T(8,128)(2,1)}, u32[]{:S(2)}, u32[]{:S(2)}) async-start(bf16[128,40,1280]{2,1,0:T(8,128)(2,1)} %bitcast.109), calls=%async_computation.2 | async-start | bytes 26214400 | tf_op jit(solution)/shard_map/all_to_all | solution.py:30
  931.7 8.8 convert_reduce_fusion
  940.6 8.9 convert_reduce_fusion.1
  950.2 6.5 convert_reduce_fusion.2
  956.8 149.7 %all-to-all-done.2 = bf16[128,40,1280]{2,1,0:T(8,128)(2,1)} async-done(((bf16[128,40,1280]{2,1,0:T(8,128)(2,1)}), bf16[128,40,1280]{2,1,0:T(8,128)(2,1)}, u32[]{:S(2)}, u32[]{:S(2)}) %all-to-all-start.2) | async-done | bytes 13107232 | tf_op jit(solution)/shard_map/all_to_all | solution.py:30
  1106.5 6.5 convert_reduce_fusion.3
  1115.0 79.3 %psum.7 = f32[]{:T(128)} all-reduce(f32[]{:T(128)S(6)} %add.83), channel_id=1, replica_groups=mesh['fsdp'=128] {'fsdp'}, use_global_device_ids=true, to_apply=%region_6.0 | all-reduce | flops 1 | bytes 8 | tf_op jit(solution)/shard_map/psum | solution.py:56
  1195.0 2.3 fusion.166
  1198.1 2.0 fusion.163
  1202.6 1.1 copy.38
  1205.8 62.9 %all-gather.11.cloned.1.call-done = bf16[1,5120,1280]{2,1,0:T(8,128)(2,1)} async-done(((bf16[1,40,1280]{2,1,0:T(8,128)(2,1)}), bf16[1,5120,1280]{2,1,0:T(8,128)(2,1)}) %all-gather.11.cloned.1.call-update) | async-done | bytes 13107216 | tf_op jit(solution)/shard_map/all_gather | solution.py:73
  1268.7 97.7 %all-gather.9.cloned.1.call-done = bf16[1,1280,5120]{2,0,1:T(2,128)(2,1)} async-done(((bf16[1,10,5120]{2,0,1:T(2,128)(2,1)}), bf16[1,1280,5120]{2,0,1:T(2,128)(2,1)}) %all-gather.9.cloned.1.call-update) | async-done | bytes 13107216 | tf_op jit(solution)/shard_map/all_gather | solution.py:72
  1366.4 26.6 %fusion.114 = bf16[384,1280]{1,0:T(8,128)(2,1)S(1)} fusion(bf16[1,5120,1280]{2,1,0:T(8,128)(2,1)} %all-gather.11.cloned.1.call-done, bf16[1,1280,5120]{2,0,1:T(2,128)(2,1)} %all-gather.9.cloned.1.call-done, bf16[1,384,1280]{2,1,0:T(8,128)(2,1)} %param.15), kind=kOutput, calls=%fused_computation.100 | convolution fusion | flops 10085498880 | bytes 28180480 | tf_op jit(solution)/shard_map/dot_general | solution.py:76
  1393.0 49.7 %all-gather.15.cloned.1.call-done = bf16[1,5120,1280]{2,1,0:T(8,128)(2,1)} async-done(((bf16[1,40,1280]{2,1,0:T(8,128)(2,1)}), bf16[1,5120,1280]{2,1,0:T(8,128)(2,1)}) %all-gather.15.cloned.1.call-update) | async-done | bytes 13107216 | tf_op jit(solution)/shard_map/all_gather | solution.py:73
  1442.7 96.9 %all-gather.13.cloned.1.call-done = bf16[1,1280,5120]{2,0,1:T(2,128)(2,1)} async-done(((bf16[1,10,5120]{2,0,1:T(2,128)(2,1)}), bf16[1,1280,5120]{2,0,1:T(2,128)(2,1)}) %all-gather.13.cloned.1.call-update) | async-done | bytes 13107216 | tf_op jit(solution)/shard_map/all_gather | solution.py:72
  1539.6 21.0 %fusion.119 = bf16[1,384,1280]{2,1,0:T(8,128)(2,1)} fusion(bf16[1,5120,1280]{2,1,0:T(8,128)(2,1)} %all-gather.15.cloned.1.call-done, bf16[384,1280]{1,0:T(8,128)(2,1)S(1)} %fusion.114, bf16[1,1280,5120]{2,0,1:T(2,128)(2,1)} %all-gather.13.cloned.1.call-done), kind=kOutput, calls=%fused_computation.101 | convolution fusion | flops 10085498880 | bytes 28180480 | tf_op jit(solution)/shard_map/dot_general | solution.py:76
  (36 shorter events, 7.2 us)
Async XLA Ops:
  7.2 8.6 copy-start.6
  15.8 15.9 %copy-start.7 = (f32[384,5120]{1,0:T(8,128)}, f32[384,5120]{1,0:T(8,128)S(1)}, u32[]{:S(2)}) copy-start(f32[384,5120]{1,0:T(8,128)S(1)} %fusion.18) | copy-start | bytes 23592964
  15.8 15.9 %copy-start.5 = (bf16[2,1,384,1280]{3,2,1,0:T(8,128)(2,1)S(1)}, bf16[2,1,384,1280]{3,2,1,0:T(8,128)(2,1)}, u32[]{:S(2)}) copy-start(bf16[2,1,384,1280]{3,2,1,0:T(8,128)(2,1)} %param.13) | copy-start | bytes 5898244
  67.8 316.2 %all-to-all-start.1 = ((bf16[128,10,5120]{2,1,0:T(8,128)(2,1)}), bf16[128,10,5120]{2,1,0:T(8,128)(2,1)}, u32[]{:S(2)}, u32[]{:S(2)}) async-start(bf16[128,10,5120]{2,1,0:T(8,128)(2,1)} %all_to_all.26), calls=%async_computation.1 | async-start | bytes 41943040 | tf_op jit(solution)/shard_map/all_to_all | solution.py:30
  80.0 12.3 copy-start.8
  384.0 327.6 %all-to-all-start = ((bf16[128,10,5120]{2,1,0:T(8,128)(2,1)}), bf16[128,10,5120]{2,1,0:T(8,128)(2,1)}, u32[]{:S(2)}, u32[]{:S(2)}) async-start(bf16[128,10,5120]{2,1,0:T(8,128)(2,1)} %all_to_all.24), calls=%async_computation | async-start | bytes 41943040 | tf_op jit(solution)/shard_map/all_to_all | solution.py:30
  711.6 23.4 %copy-start.9 = (bf16[384,1280]{1,0:T(8,128)(2,1)S(1)}, bf16[384,1280]{1,0:T(8,128)(2,1)}, u32[]{:S(2)}) copy-start(bf16[384,1280]{1,0:T(8,128)(2,1)} %fusion.106) | copy-start | bytes 2949124
  711.6 198.4 %all-to-all-start.3 = ((bf16[128,40,1280]{2,1,0:T(8,128)(2,1)}), bf16[128,40,1280]{2,1,0:T(8,128)(2,1)}, u32[]{:S(2)}, u32[]{:S(2)}) async-start(bf16[128,40,1280]{2,1,0:T(8,128)(2,1)} %bitcast.110), calls=%async_computation.3 | async-start | bytes 26214400 | tf_op jit(solution)/shard_map/all_to_all | solution.py:30
  910.0 196.5 %all-to-all-start.2 = ((bf16[128,40,1280]{2,1,0:T(8,128)(2,1)}), bf16[128,40,1280]{2,1,0:T(8,128)(2,1)}, u32[]{:S(2)}, u32[]{:S(2)}) async-start(bf16[128,40,1280]{2,1,0:T(8,128)(2,1)} %bitcast.109), calls=%async_computation.2 | async-start | bytes 26214400 | tf_op jit(solution)/shard_map/all_to_all | solution.py:30
  931.5 337.3 %all-gather.11.cloned.1.call-start = ((), (), s32[]{:S(2)}) async-start(), calls=%async_computation.5 | async-start | bytes 13209600 | tf_op jit(solution)/shard_map/all_gather | solution.py:73
  940.6 8.9 copy-start
  956.7 156.3 %copy-start.1 = (f32[2,40,1280]{2,1,0:T(8,128)S(1)}, f32[2,40,1280]{2,1,0:T(8,128)}, u32[]{:S(2)}) copy-start(f32[2,40,1280]{2,1,0:T(8,128)} %param.19) | copy-start | bytes 1228804
  956.7 238.3 %copy-start.3 = (f32[2,40,1280]{2,1,0:T(8,128)S(1)}, f32[2,40,1280]{2,1,0:T(8,128)}, u32[]{:S(2)}) copy-start(f32[2,40,1280]{2,1,0:T(8,128)} %param.21) | copy-start | bytes 1228804
  956.8 238.3 %copy-start.4 = (f32[2,40,1280]{2,1,0:T(8,128)S(1)}, f32[2,40,1280]{2,1,0:T(8,128)}, u32[]{:S(2)}) copy-start(f32[2,40,1280]{2,1,0:T(8,128)} %param.23) | copy-start | bytes 1228804
  956.8 241.3 %copy-start.2 = (f32[2,10,5120]{2,0,1:T(2,128)S(1)}, f32[2,10,5120]{2,0,1:T(2,128)}, u32[]{:S(2)}) copy-start(f32[2,10,5120]{2,0,1:T(2,128)} %param.20) | copy-start | bytes 1228804
  1198.0 168.4 %all-gather.9.cloned.1.call-start = ((), (), s32[]{:S(2)}) async-start(), calls=%async_computation.4 | async-start | bytes 26419200 | tf_op jit(solution)/shard_map/all_gather | solution.py:72
  1201.0 241.7 %all-gather.15.cloned.1.call-start = ((), (), s32[]{:S(2)}) async-start(), calls=%async_computation.7 | async-start | bytes 13209600 | tf_op jit(solution)/shard_map/all_gather | solution.py:73
  1201.7 337.9 %all-gather.13.cloned.1.call-start = ((), (), s32[]{:S(2)}) async-start(), calls=%async_computation.6 | async-start | bytes 26419200 | tf_op jit(solution)/shard_map/all_gather | solution.py:72
Sparse Core Ops, SparseCore 0:
  1198.1 70.5 all-gather.10
  1272.3 94.0 all-gather.8
  1369.3 73.2 all-gather.14
  1445.5 94.0 all-gather.12
where the time goes:
time: 1580 us; the launch traced here: 1570 us
  waiting for transfers between devices  1140 us (72%)
  matrix products  157 us (10%)
  starting transfers between devices  80.8 us (5%)
  blocking collectives  79.3 us (5%)
  local copies, waits for them, and re-layouts  53.6 us (3%)
  other arithmetic  36.5 us (2%)
  between operations  16.4 us (1%)
    all_to_all x4, waiting for transfers between devices, reduce_rows(): received = lax.all_to_all(part_grad, 'fsdp', 0, 0, tiled=True)  836 us
    all_gather x2, waiting for transfers between devices, local_step(): w_layer_up = lax.all_gather(up_shard[layer_idx], 'fsdp', axis=0, tiled=True)  195 us
    all_gather x2, waiting for transfers between devices, local_step(): lax.all_gather(down_shard[layer_idx], 'fsdp', axis=0, tiled=True)  113 us
    all_to_all x4, starting transfers between devices, reduce_rows(): received = lax.all_to_all(part_grad, 'fsdp', 0, 0, tiled=True)  80.5 us
    psum x1, blocking collectives, backward_update(): lax.psum(local_sq, 'fsdp')  79.3 us
    all_to_all x2, local copies, waits for them, and re-layouts, reduce_rows(): received = lax.all_to_all(part_grad, 'fsdp', 0, 0, tiled=True)  47.9 us
    dot_general x2, matrix products, local_step(): jnp.dot(hidden_act, w_layer_down, preferred_element_type=jnp.float32)  47.6 us
    dot_general x2, matrix products, backward_update(): lax.dot_general(x_in, d_pre, (((0,), (0,)), ((), ())), preferred_element_...  32.1 us
  transfers between devices with their start and end apart: 8, of which 8 were waited for; matrix products, arithmetic and copies ran while one was open for 8% of the time, Pallas kernels for 0%

commit v1 on v0

v1 whole, which is shorter than its diff:
```python
import functools
import math

import jax
import jax.numpy as jnp
from jax import lax
from jax.experimental import pallas as pl
from jax.experimental.pallas import tpu as pltpu
from jax.sharding import PartitionSpec as P

LEARN_RATE = 0.001
BETA_ONE = 0.9
BETA_TWO = 0.95
ADAM_EPS = 1e-8
WEIGHT_DECAY = 0.1
ADAM_STEP = 3
MICRO_STEPS = 2

MESH = pl.DeviceIdType.MESH
BF16 = jnp.bfloat16
F32 = jnp.float32
VMEM_LIMIT = 67_000_000
LAYERS = 2
RING = 4
WIDTH = 1280
FF = 5120
UP_ROWS = 10
DOWN_ROWS = 40
BLOCK = 80
COLS = 640
PAIR_ROWS = 2 * BLOCK
ROWS = LAYERS * PAIR_ROWS
LANES = 128
OCTET = 8
CHUNK = 8
SEMS = pltpu.SemaphoreType.DMA

BATCH_CHUNKS = PAIR_ROWS // CHUNK
ORDERS = ((0, 1, 2), (1, 2, 0), (2, 0, 1))
N_FLOWS = 6
FLOWS = range(N_FLOWS)
TICKS = RING
STEPS = RING - 1
BATCH_LEN = [[TICKS if f // 2 == b else TICKS - 1 for f in FLOWS] for b in range(LAYERS)]
BATCH_START = [[sum(lens[:f]) for f in FLOWS] for lens in BATCH_LEN]
OWN_SLOTS = 3
UP_TILES = 8
TILES = 16


def up_base(layer):
    return (LAYERS - 1 - layer) * PAIR_ROWS


def down_base(layer):
    return up_base(layer) + BLOCK


def comm_params(collective_id):
    return pltpu.CompilerParams(collective_id=collective_id, has_side_effects=True, vmem_limit_bytes=VMEM_LIMIT)


def plain_params(dims):
    return pltpu.CompilerParams(dimension_semantics=("arbitrary",) * dims, vmem_limit_bytes=VMEM_LIMIT)


def in_vmem():
    return pl.BlockSpec(memory_space=pltpu.VMEM)


def in_hbm():
    return pl.BlockSpec(memory_space=pl.ANY)


def aligned(start, size):
    return pl.ds(pl.multiple_of(start, CHUNK), size)


def aligned_lanes(start, size):
    return pl.ds(pl.multiple_of(start, LANES), size)


def remote(src, dst, send, got, device):
    return pltpu.make_async_remote_copy(
        src_ref=src, dst_ref=dst, send_sem=send, recv_sem=got, device_id=(device,), device_id_type=MESH
    )

def flow_dims(flow):
    return ORDERS[flow // 2]


def flow_sign(flow):
    return 1 - 2 * (flow % 2)


def my_place():
    me = lax.axis_index("fsdp")
    core, chip = lax.rem(me, 2), lax.div(me, 2)
    line = lax.div(chip, RING)
    return core, (lax.div(line, RING), lax.rem(line, RING), lax.rem(chip, RING))


def device_at(pos, core):
    return ((pos[0] * RING + pos[1]) * RING + pos[2]) * 2 + core


def neighbor(pos, core, dim, sign):
    moved = list(pos)
    moved[dim] = lax.rem(pos[dim] + RING + sign, RING)
    return device_at(moved, core)


def all_neighbors(pos, core):
    return [neighbor(pos, core, dim, sign) for dim in range(3) for sign in (1, -1)]


def entry_barrier(peers):
    barrier = pltpu.get_barrier_semaphore()
    for peer in peers:
        pl.semaphore_signal(barrier, inc=1, device_id=(peer,), device_id_type=MESH)
    pl.semaphore_wait(barrier, len(peers))


def rounded_product(left, right):
    return lax.dot_general(left, right, (((0,), (0,)), ((), ())), preferred_element_type=F32).astype(BF16).astype(F32)


def reduce_kernel(
    s_last, x_own, d_own, a_own, g_own, out_ref, s_first, x_pair, d_pair, a_pair, g_pair,
    recv1, recv2, recv3, own, left, left_pair, right, right_pair, tile, own_sem, tile_in, tile_out, pair_send, pair_got, credit,
    send1, got1, send2, got2, send3, got3,
):
    core, pos = my_place()
    partner = device_at(pos, 1 - core)
    entry_barrier([partner] + all_neighbors(pos, core))
    target = [[neighbor(pos, core, dim, flow_sign(f)) for dim in flow_dims(f)] for f in FLOWS]
    source = [neighbor(pos, core, flow_dims(f)[0], -flow_sign(f)) for f in FLOWS]
    sums = (s_last, s_first)

    def seg(flow, phase, step):
        at = pos[flow_dims(flow)[phase]]
        return lax.rem(at + 2 * RING - flow_sign(flow) * (1 + step), RING)

    def s_slice(b, flow, j, chunk):
        index = [slice(None)] * 3
        index[flow_dims(flow)[0]] = j
        return sums[b].at[(*index, aligned(chunk * CHUNK, CHUNK), slice(None))]

    def part2(flow, ref, j):
        second, third = flow_dims(flow)[1:]
        return ref.at[j] if second < third else ref.at[:, j]

    def slot1(b, step):
        return step + b * 2 * ((step + 1) // 2)

    def land1(b, step, chunk):
        return recv1.at[slot1(b, step), chunk]

    def land2(b, step, chunk):
        return recv2.at[b, step, chunk]

    def land3(b, step, chunk):
        return recv3.at[b, step, chunk]

    lands, sends, gots = (land1, land2, land3), (send1, send2, send3), (got1, got2, got3)

    def copy(phase, b, flow, step, chunk, src):
        dst = lands[phase](b, step, chunk)
        return remote(dst if src is None else src, dst, sends[phase].at[b, step, chunk], gots[phase].at[b, step, chunk], target[flow][phase])

    def first_copy(phase, b, flow, chunk):
        j = seg(flow, phase, 0)
        if phase == 0:
            src = s_slice(b, flow, j, chunk)
        elif phase == 1:
            src = part2(flow, land1(b, STEPS - 1, chunk), j)
        else:
            src = recv2.at[b, STEPS - 1, chunk, j]
        return copy(phase, b, flow, 0, chunk, src)

    def next_copy(phase, b, flow, step, chunk):
        return copy(phase, b, flow, step + 1, chunk, lands[phase](b, step, chunk))

    def own_copy(b, flow, n):
        step, k = lax.div(n, TICKS), lax.rem(n, TICKS)
        slot = lax.rem(n, OWN_SLOTS)
        src = s_slice(b, flow, seg(flow, 0, step + 1), BATCH_START[b][flow] + k)
        return pltpu.make_async_copy(src, own.at[flow, slot], own_sem.at[flow, slot])

    def start_batch(b):
        for k in range(TICKS):
            for f in FLOWS:
                if k < BATCH_LEN[b][f]:
                    first_copy(0, b, f, BATCH_START[b][f] + k).start()
        for n in range(OWN_SLOTS - 1):
            for f in FLOWS:
                own_copy(b, f, n).start()

    def tick(phase, b, n):
        step, k = lax.div(n, TICKS), lax.rem(n, TICKS)

        def each(body):
            for f in FLOWS:
                if BATCH_LEN[b][f] == TICKS:
                    body(f, BATCH_START[b][f] + k)
                else:
                    pl.when(k < BATCH_LEN[b][f])(functools.partial(body, f, BATCH_START[b][f] + k))

        def add(f, chunk):
            copy(phase, b, f, step, chunk, None).wait_recv()
            landed = lands[phase](b, step, chunk)
            if phase == 0:
                own_copy(b, f, n).wait()
                landed[...] = landed[...] + own[f, lax.rem(n, OWN_SLOTS)]
            elif phase == 1:
                landed[...] = landed[...] + part2(f, land1(b, STEPS - 1, chunk), seg(f, 1, step + 1))[...]
            else:
                landed[...] = landed[...] + recv2[b, STEPS - 1, chunk, seg(f, 2, step + 1)]

        def pass_on(f, chunk):
            @pl.when(step < STEPS - 1)
            def _():
                next_copy(phase, b, f, step, chunk).start()

            @pl.when(step == STEPS - 1)
            def _():
                if phase < 2:
                    first_copy(phase + 1, b, f, chunk).start()
                else:
                    out_ref[aligned((b * BATCH_CHUNKS + chunk) * CHUNK, CHUNK), :] = recv3[b, STEPS - 1, chunk]

        if phase == 0:
            later = n + OWN_SLOTS - 1
            for f in FLOWS:
                @pl.when((later < STEPS * TICKS) & (lax.rem(later, TICKS) < BATCH_LEN[b][f]))
                def _():
                    own_copy(b, f, later).start()

        each(add)
        each(pass_on)

    def tile_reads(job, up):
        slot = lax.rem(job, 2)
        if up:
            rows = aligned_lanes(lax.div(job, RING) * COLS, COLS)
            cols = lax.rem(job, RING) * COLS
            reads = (x_own.at[:, rows], x_pair.at[:, rows], d_own.at[:, aligned_lanes(core * (FF // 2) + cols, COLS)], d_pair.at[:, aligned_lanes(cols, COLS)])
        else:
            rows = aligned_lanes((job - UP_TILES) * COLS, COLS)
            reads = (a_own.at[:, rows], a_pair.at[:, rows], g_own.at[:, aligned_lanes(core * COLS, COLS)], g_pair)
        return [
            pltpu.make_async_copy(src, dst.at[slot], tile_in.at[i, slot])
            for i, (src, dst) in enumerate(zip(reads, (left, left_pair, right, right_pair)))
        ]

    def start_reads(job):
        for up in (True, False):
            @pl.when((job < UP_TILES) if up else (job >= UP_TILES) & (job < TILES))
            def _():
                for read in tile_reads(job, up):
                    read.start()

    def tile_write(job, up):
        slot = lax.rem(job, 2)
        if up:
            dst = s_first.at[pl.ds(lax.div(job, RING) * 2, 2), :, lax.rem(job, RING), pl.ds(0, BLOCK)]
        else:
            i = job - UP_TILES
            dst = s_first.at[lax.div(i, 2), pl.ds(lax.rem(i, 2) * 2, 2), :, pl.ds(BLOCK, BLOCK)]
        return pltpu.make_async_copy(tile.at[slot], dst, tile_out.at[slot])

    def compute(job):
        slot = lax.rem(job, 2)
        start_reads(job + 1)
        for read in tile_reads(UP_TILES + slot, False):
            read.wait()

        @pl.when(job >= 2)
        def _():
            tile_write(UP_TILES + slot, False).wait()

        total = rounded_product(left[slot], right[slot]) + rounded_product(left_pair[slot], right_pair[slot])
        tile[slot] = total.reshape(tile.shape[1:])
        for up in (True, False):
            @pl.when((job < UP_TILES) if up else (job >= UP_TILES))
            def _():
                tile_write(job, up).start()

    start_batch(0)
    other = 1 - core
    gives = (x_own, d_own.at[:, aligned_lanes(other * (FF // 2), FF // 2)], a_own, g_own.at[:, aligned_lanes(other * COLS, COLS)])
    exchange = [
        remote(src, dst, pair_send.at[i], pair_got.at[i], partner)
        for i, (src, dst) in enumerate(zip(gives, (x_pair, d_pair, a_pair, g_pair)))
    ]
    for give in exchange:
        give.start()
    for give in exchange:
        give.wait_recv()
    start_reads(0)

    @pl.loop(0, 2 * TICKS)
    def _(n):
        tick(0, 0, n)

        @pl.loop(0, 2)
        def _(i):
            compute(2 * n + i)

    for slot in range(2):
        tile_write(UP_TILES + slot, False).wait()
    for f in FLOWS:
        for k in range(BATCH_LEN[0][f]):
            copy(0, 0, f, 1, BATCH_START[0][f] + k, None).wait_send()
        pl.semaphore_signal(credit.at[f], inc=1, device_id=(source[f],), device_id_type=MESH)
    for f in FLOWS:
        pl.semaphore_wait(credit.at[f], 1)
    for k in range(TICKS):
        for f in FLOWS:
            if k < BATCH_LEN[1][f]:
                first_copy(0, 1, f, BATCH_START[1][f] + k).start()

    @pl.loop(2 * TICKS, STEPS * TICKS)
    def _(n):
        tick(0, 0, n)

    for n in range(OWN_SLOTS - 1):
        for f in FLOWS:
            own_copy(1, f, n).start()

    @pl.loop(0, STEPS * TICKS)
    def _(n):
        tick(0, 1, n)
        tick(1, 0, n)

    @pl.loop(0, STEPS * TICKS)
    def _(n):
        tick(1, 1, n)
        tick(2, 0, n)

    @pl.loop(0, STEPS * TICKS)
    def _(n):
        tick(2, 1, n)

    for give in exchange:
        give.wait_send()
    for b in range(LAYERS):
        for f in FLOWS:
            @pl.loop(BATCH_START[b][f], BATCH_START[b][f] + BATCH_LEN[b][f])
            def _(chunk):
                for phase in range(3):
                    for step in range(STEPS):
                        if (phase, b, step) != (0, 0, 1):
                            copy(phase, b, f, step, chunk, None).wait_send()


def reduce_blocks(s_last, x_first, d_first, a_first, g_first):
    tokens = x_first.shape[0]

    def half(width):
        return jax.ShapeDtypeStruct((tokens, width), BF16)

    piece = pltpu.VMEM((2, tokens, COLS), BF16)
    sems = SEMS((LAYERS, STEPS, BATCH_CHUNKS))
    return pl.pallas_call(
        reduce_kernel,
        out_shape=[jax.ShapeDtypeStruct((ROWS, COLS), F32), jax.ShapeDtypeStruct(s_last.shape, F32), half(WIDTH), half(FF // 2), half(FF), half(COLS)],
        in_specs=[in_hbm()] * 5,
        out_specs=[in_vmem()] + [in_hbm()] * 5,
        scratch_shapes=[
            pltpu.VMEM((5, BATCH_CHUNKS, RING, RING, CHUNK, COLS), F32),
            pltpu.VMEM((LAYERS, STEPS, BATCH_CHUNKS, RING, CHUNK, COLS), F32),
            pltpu.VMEM((LAYERS, STEPS, BATCH_CHUNKS, CHUNK, COLS), F32),
            pltpu.VMEM((N_FLOWS, OWN_SLOTS, RING, RING, CHUNK, COLS), F32),
            piece, piece, piece, piece,
            pltpu.VMEM((2, 2, RING, BLOCK, COLS), F32),
            SEMS((N_FLOWS, OWN_SLOTS)), SEMS((4, 2)), SEMS((2,)), SEMS((4,)), SEMS((4,)), pltpu.SemaphoreType.REGULAR((N_FLOWS,)),
            sems, sems, sems, sems, sems, sems,
        ],
        compiler_params=comm_params(1),
        name="torus_reduce",
    )(s_last, x_first, d_first, a_first, g_first)[0]


GATHER_LEN = [BATCH_LEN[0][f] + BATCH_LEN[1][f] for f in FLOWS]
GATHER_START = [sum(GATHER_LEN[:f]) for f in FLOWS]


def gather_kernel(block_ref, all_ref, own_sem, send1, got1, send2, got2, send3, got3, pair_send, pair_got):
    core, pos = my_place()
    partner = device_at(pos, 1 - core)
    entry_barrier([partner] + all_neighbors(pos, core))
    target = [[neighbor(pos, core, dim, flow_sign(f)) for dim in flow_dims(f)] for f in FLOWS]

    def flow_rows(flow):
        return pl.ds(GATHER_START[flow] * CHUNK, GATHER_LEN[flow] * CHUNK)

    def back(flow, phase, steps):
        at = pos[flow_dims(flow)[phase]]
        return lax.rem(at + RING - flow_sign(flow) * steps, RING)

    def place(flow, first, second, third):
        index = [None] * 3
        for dim, at in zip(flow_dims(flow), (first, second, third)):
            index[dim] = at
        return all_ref.at[(core, *index, flow_rows(flow), slice(None))]

    def copy1(flow, step):
        ref = place(flow, back(flow, 0, step), back(flow, 1, 0), back(flow, 2, 0))
        if step == 0:
            return remote(block_ref.at[flow_rows(flow)], ref, send1.at[flow, step], got1.at[flow, step], target[flow][0])
        return remote(ref, ref, send1.at[flow, step], got1.at[flow, step], target[flow][0])

    def wait1(flow, step):
        ref = place(flow, back(flow, 0, step + 1), back(flow, 1, 0), back(flow, 2, 0))
        remote(ref, ref, send1.at[flow, step], got1.at[flow, step], target[flow][0]).wait_recv()

    def copy2(flow, step, u, off=0):
        ref = place(flow, back(flow, 0, u), back(flow, 1, step + off), back(flow, 2, 0))
        if step == 0 and u == 0 and off == 0:
            return remote(block_ref.at[flow_rows(flow)], ref, send2.at[flow, step, u], got2.at[flow, step, u], target[flow][1])
        return remote(ref, ref, send2.at[flow, step, u], got2.at[flow, step, u], target[flow][1])

    def copy3(flow, step, v, off=0):
        ref = place(flow, slice(None), back(flow, 1, v), back(flow, 2, step + off))
        return remote(ref, ref, send3.at[flow, step, v], got3.at[flow, step, v], target[flow][2])

    def pair_copy(flow, w, v):
        ref = place(flow, slice(None), back(flow, 1, v), back(flow, 2, w))
        return remote(ref, ref, pair_send.at[flow, w, v], pair_got.at[flow, w, v], partner)

    def pair_wait(flow, w, v):
        index = [None] * 3
        for dim, at in zip(flow_dims(flow), (slice(None), back(flow, 1, v), back(flow, 2, w))):
            index[dim] = at
        ref = all_ref.at[(1 - core, *index, flow_rows(flow), slice(None))]
        remote(ref, ref, pair_send.at[flow, w, v], pair_got.at[flow, w, v], partner).wait_recv()

    flows = FLOWS
    local = pltpu.make_async_copy(block_ref, all_ref.at[core, pos[0], pos[1], pos[2]], own_sem)
    local.start()
    for f in flows:
        copy1(f, 0).start()
    for f in flows:
        copy2(f, 0, 0).start()
    local.wait()
    for step in range(STEPS):
        for f in flows:
            wait1(f, step)
            if step < STEPS - 1:
                copy1(f, step + 1).start()
            copy2(f, 0, step + 1).start()
    for f in flows:
        copy3(f, 0, 0).start()
        pair_copy(f, 0, 0).start()
    for step in range(STEPS):
        for u in range(RING):
            for f in flows:
                copy2(f, step, u, 1).wait_recv()
                if step < STEPS - 1:
                    copy2(f, step + 1, u).start()
                if u == RING - 1:
                    copy3(f, 0, step + 1).start()
                    pair_copy(f, 0, step + 1).start()
    for step in range(STEPS):
        for v in range(RING):
            for f in flows:
                copy3(f, step, v, 1).wait_recv()
                if step < STEPS - 1:
                    copy3(f, step + 1, v).start()
                pair_copy(f, step + 1, v).start()
    for w in range(RING):
        for v in range(RING):
            for f in flows:
                pair_wait(f, w, v)
    for f in flows:
        for step in range(STEPS):
            copy1(f, step).wait_send()
            for u in range(RING):
                copy2(f, step, u).wait_send()
                copy3(f, step, u).wait_send()
        for w in range(RING):
            for v in range(RING):
                pair_copy(f, w, v).wait_send()


def gather_blocks(block):
    one, four, pair = SEMS((N_FLOWS, STEPS)), SEMS((N_FLOWS, STEPS, RING)), SEMS((N_FLOWS, RING, RING))
    return pl.pallas_call(
        gather_kernel,
        out_shape=jax.ShapeDtypeStruct((2, RING, RING, RING, ROWS, COLS), BF16),
        in_specs=[in_vmem()],
        out_specs=in_hbm(),
        scratch_shapes=[SEMS, one, one, four, four, four, four, pair, pair],
        compiler_params=comm_params(2),
        name="torus_gather",
    )(block)


def grad_kernel(core_ref, left, left_pair, right, right_pair, *refs):
    del core_ref
    out = refs[-1]
    total = rounded_product(left[...], right[...]) + rounded_product(left_pair[...], right_pair[...])
    if total.shape[1] == COLS:
        out[...] = total.reshape(out.shape)
    else:
        for x in range(out.shape[1]):
            out[:, x, 0] = total[:, COLS * x:COLS * (x + 1)].reshape(-1, BLOCK, COLS)


def grad_sum(core, left, left_pair, right, right_pair, sums):
    tokens = left.shape[0]
    zy = RING * RING
    if sums is None:
        grid = (2, 2)
        left_spec = pl.BlockSpec((tokens, COLS), lambda i, x, c: (0, i))
        right_spec = pl.BlockSpec((tokens, 2 * COLS), lambda i, x, c: (0, c[0] * 2 + x))
        out_spec = pl.BlockSpec((zy // 2, 2, 1, BLOCK, COLS), lambda i, x, c: (i, x, 0, 0, 0))
    else:
        grid = (FF // COLS,)
        left_spec = pl.BlockSpec((tokens, COLS), lambda i, c: (0, i))
        right_spec = pl.BlockSpec((tokens, COLS), lambda i, c: (0, c[0]))
        out_spec = pl.BlockSpec((2, RING, 1, BLOCK, COLS), lambda i, c: (i, 0, 1, 0, 0))
    before = [] if sums is None else [sums]
    return pl.pallas_call(
        grad_kernel,
        out_shape=jax.ShapeDtypeStruct((zy, RING, 2, BLOCK, COLS), F32),
        grid_spec=pltpu.PrefetchScalarGridSpec(
            num_scalar_prefetch=1,
            grid=grid,
            in_specs=[left_spec, left_spec, right_spec, right_spec] + [in_hbm()] * len(before),
            out_specs=out_spec,
        ),
        input_output_aliases={5: 0} if before else {},
        compiler_params=plain_params(len(grid)),
        cost_estimate=pl.CostEstimate(flops=2 * tokens * WIDTH * FF, bytes_accessed=17_000_000, transcendentals=0),
        name="grad_up" if sums is None else "grad_down",
    )(core, left, left_pair, right, right_pair, *before)


def gelu_fn(pre_act):
    return jax.nn.gelu(pre_act, approximate=True)


def up_kernel(hidden, weight, out):
    wide = jnp.concatenate([weight[0, :, x, 0].reshape(WIDTH, COLS) for x in range(2)], axis=1)
    pre_act = jnp.dot(hidden[...], wide, preferred_element_type=F32)
    out[...] = gelu_fn(pre_act).astype(BF16)


def down_kernel(act, weight, hidden, out, total):
    step = pl.program_id(0)

    @pl.when(step == 0)
    def _():
        total[...] = hidden[...].astype(F32)

    wide = jnp.concatenate([weight[c].reshape(WIDTH, COLS) for c in range(2)], axis=1)
    total[...] += jnp.dot(act[...], wide, preferred_element_type=F32)

    @pl.when(step == pl.num_programs(0) - 1)
    def _():
        out[...] = total[...].astype(BF16)


def forward_layer(hidden, weights, layer):
    tokens = hidden.shape[0]
    act = pl.pallas_call(
        up_kernel,
        out_shape=jax.ShapeDtypeStruct((tokens, FF), BF16),
        grid=(2, 2),
        in_specs=[
            pl.BlockSpec((tokens, WIDTH), lambda c, x: (0, 0)),
            pl.BlockSpec((1, 16, 2, 1, BLOCK, COLS), lambda c, x: (c, 0, x, 2 * (LAYERS - 1 - layer), 0, 0)),
        ],
        out_specs=pl.BlockSpec((tokens, 2 * COLS), lambda c, x: (0, c * 2 + x)),
        compiler_params=plain_params(2),
        name="forward_up",
    )(hidden, weights)
    return pl.pallas_call(
        down_kernel,
        out_shape=jax.ShapeDtypeStruct((tokens, WIDTH), BF16),
        grid=(4,),
        in_specs=[
            pl.BlockSpec((tokens, WIDTH), lambda i: (0, i)),
            pl.BlockSpec((2, 4, 4, 1, BLOCK, COLS), lambda i: (0, i, 0, 2 * (LAYERS - 1 - layer) + 1, 0, 0)),
            pl.BlockSpec((tokens, WIDTH), lambda i: (0, 0)),
        ],
        out_specs=pl.BlockSpec((tokens, WIDTH), lambda i: (0, 0)),
        scratch_shapes=[pltpu.VMEM((tokens, WIDTH), F32)],
        compiler_params=plain_params(1),
        name="forward_down",
    )(act, weights, hidden)


def adamw_update(master_old, mom_one, mom_two, grad_clip):
    mom_one_new = BETA_ONE * mom_one + (1.0 - BETA_ONE) * grad_clip
    mom_two_new = BETA_TWO * mom_two + (1.0 - BETA_TWO) * grad_clip * grad_clip
    first_hat = mom_one_new / (1.0 - BETA_ONE ** ADAM_STEP)
    second_hat = mom_two_new / (1.0 - BETA_TWO ** ADAM_STEP)
    master_new = master_old - LEARN_RATE * (first_hat / (jnp.sqrt(second_hat) + ADAM_EPS) + WEIGHT_DECAY * master_old)
    return master_new, mom_one_new, mom_two_new


N_PEERS = OCTET - 1 + 2 * (RING - 1)


def update_kernel(
    block, gacc_up, gacc_down, master_up, master_down, mom1_up, mom1_down, mom2_up, mom2_down,
    new_block, master_up_new, master_down_new, mom1_up_new, mom1_down_new, mom2_up_new, mom2_down_new,
    stage_up, recv_up, recv_down, grad_up, grad_down, norm_send, norm_recv, wide, shard_up, shard_recv, shard_down,
    send_up, got_up, send_down, got_down, send_norm, got_norm, send_w, got_w, send_wd, got_wd,
):
    core, pos = my_place()
    mine = pos[2] * 2 + core
    partner = device_at(pos, 1 - core)
    octet = [(lax.rem(mine + k, OCTET), device_at((pos[0], pos[1], 0), lax.rem(mine + k, OCTET))) for k in range(1, OCTET)]
    along = [[neighbor(pos, core, dim, k) for k in range(1, RING)] for dim in (1, 0)]
    entry_barrier([device for _, device in octet] + along[0] + along[1])

    def down_copy(layer):
        rows = aligned(down_base(layer) + DOWN_ROWS * (1 - core), DOWN_ROWS)
        return remote(block.at[rows], recv_down.at[layer], send_down.at[layer], got_down.at[layer], partner)

    for layer in range(LAYERS):
        down_copy(layer).start()
    for q in range(OCTET):
        for j in range(UP_ROWS):
            for layer in range(LAYERS):
                stage_up[q, j, pl.ds(layer, 1), :] = block[pl.ds(up_base(layer) + q * UP_ROWS + j, 1), :]

    def up_copy(k):
        to, device = octet[k - 1]
        return remote(stage_up.at[to], recv_up.at[k], send_up.at[k - 1], got_up.at[k - 1], device)

    for k in range(1, OCTET):
        up_copy(k).start()
    recv_up[0] = stage_up[mine]

    total = jnp.zeros((CHUNK, LANES), F32)
    for layer in range(LAYERS):
        down_copy(layer).wait_recv()
        for from_me in (True, False):
            cols = aligned_lanes((core if from_me else 1 - core) * COLS, COLS)
            if from_me:
                part = block[aligned(down_base(layer) + DOWN_ROWS * core, DOWN_ROWS), :]
            else:
                part = recv_down[layer]
            grad = (gacc_down[layer, :, cols] + part) / MICRO_STEPS
            grad_down[layer, :, cols] = grad
            square = grad * grad
            for i in range(COLS // LANES):
                for n in range(COLS // LANES):
                    total = total + square[CHUNK * i:CHUNK * i + CHUNK, LANES * n:LANES * n + LANES]
    total_up = jnp.zeros((LAYERS, LANES), F32)
    for k in range(OCTET):
        if k > 0:
            up_copy(k).wait_recv()
        source = lax.rem(mine + OCTET - k, OCTET)
        cols = aligned_lanes((lax.rem(source, 2) * RING + lax.div(source, 2)) * COLS, COLS)
        for j in range(UP_ROWS):
            grad = (gacc_up[j, :, cols] + recv_up[k, j]) / MICRO_STEPS
            grad_up[j, :, cols] = grad
            square = grad * grad
            for n in range(COLS // LANES):
                total_up = total_up + square[:, LANES * n:LANES * n + LANES]
    norm_send[0] = total + jnp.concatenate([total_up, jnp.zeros((CHUNK - LAYERS, LANES), F32)], axis=0)

    slot = 0
    rounds = ([device for _, device in octet], along[0], along[1])
    sent = []
    for r, peers in enumerate(rounds):
        copies = [
            remote(norm_send.at[r], norm_recv.at[slot + k], send_norm.at[slot + k], got_norm.at[slot + k], device)
            for k, device in enumerate(peers)
        ]
        for copy in copies:
            copy.start()
        total = norm_send[r]
        for k, copy in enumerate(copies):
            copy.wait_recv()
            total = total + norm_recv[slot + k]
        slot += len(peers)
        sent += copies
        if r < 2:
            norm_send[r + 1] = total
    norm_sq = jnp.sum(total, keepdims=True)
    clip_norm = 0.1 * math.sqrt(2 * LAYERS * WIDTH * FF)
    clip = jnp.minimum(1.0, clip_norm / jnp.sqrt(norm_sq))

    for layer in range(LAYERS):
        new = adamw_update(master_down[layer], mom1_down[layer], mom2_down[layer], grad_down[layer] * clip)
        master_down_new[layer], mom1_down_new[layer], mom2_down_new[layer] = new
        weight = new[0].astype(BF16).astype(F32)
        for half in range(LAYERS):
            shard_down[half, layer] = weight[:, half * COLS:half * COLS + COLS]

    def wd_copy(layer):
        rows = aligned(down_base(layer) + DOWN_ROWS * core, DOWN_ROWS)
        return remote(shard_down.at[1 - core, layer], wide.at[rows], send_wd.at[layer], got_wd.at[layer], partner)

    for q in range(OCTET):
        cols = pl.ds(((q % 2) * RING + q // 2) * COLS, COLS)
        for j in range(UP_ROWS):
            new = adamw_update(master_up[j, :, cols], mom1_up[j, :, cols], mom2_up[j, :, cols], grad_up[j, :, cols] * clip)
            master_up_new[j, :, cols], mom1_up_new[j, :, cols], mom2_up_new[j, :, cols] = new
            shard_up[q, j] = new[0].astype(BF16).astype(F32)

    def w_copy(k):
        to, device = octet[k - 1]
        return remote(shard_up.at[to], shard_recv.at[k], send_w.at[k - 1], got_w.at[k - 1], device)

    for layer in range(LAYERS):
        wd_copy(layer).start()
    for k in range(1, OCTET):
        w_copy(k).start()
    shard_recv[0] = shard_up[mine]
    for layer in range(LAYERS):
        wide[aligned(down_base(layer) + DOWN_ROWS * core, DOWN_ROWS), :] = shard_down[core, layer]
    for k in range(OCTET):
        if k > 0:
            w_copy(k).wait_recv()
    for q in range(OCTET):
        behind = lax.rem(mine + OCTET - q, OCTET)
        for j in range(UP_ROWS):
            for layer in range(LAYERS):
                wide[pl.ds(up_base(layer) + q * UP_ROWS + j, 1), :] = shard_recv[behind, j, pl.ds(layer, 1), :]
    for layer in range(LAYERS):
        rows = aligned(down_base(layer) + DOWN_ROWS * (1 - core), DOWN_ROWS)
        remote(shard_down.at[1 - core, layer], wide.at[rows], send_wd.at[layer], got_wd.at[layer], partner).wait_recv()
    new_block[...] = wide[...].astype(BF16)

    for layer in range(LAYERS):
        down_copy(layer).wait_send()
        wd_copy(layer).wait_send()
    for k in range(1, OCTET):
        up_copy(k).wait_send()
        w_copy(k).wait_send()
    for copy in sent:
        copy.wait_send()


UP_SHAPE = (UP_ROWS, LAYERS, FF)
DOWN_SHAPE = (LAYERS, DOWN_ROWS, WIDTH)


def update_rows(block, *arrays):
    up = jax.ShapeDtypeStruct(UP_SHAPE, F32)
    down = jax.ShapeDtypeStruct(DOWN_SHAPE, F32)
    rows = pltpu.VMEM((OCTET, UP_ROWS, LAYERS, COLS), F32)
    seven, two, norm = SEMS((OCTET - 1,)), SEMS((LAYERS,)), SEMS((N_PEERS,))
    return pl.pallas_call(
        update_kernel,
        out_shape=[jax.ShapeDtypeStruct((ROWS, COLS), BF16), up, down, up, down, up, down],
        in_specs=[in_vmem()] * (1 + len(arrays)),
        out_specs=[in_vmem()] * 7,
        scratch_shapes=[
            rows, rows, pltpu.VMEM((LAYERS, DOWN_ROWS, COLS), F32), pltpu.VMEM(UP_SHAPE, F32), pltpu.VMEM(DOWN_SHAPE, F32),
            pltpu.VMEM((3, CHUNK, LANES), F32), pltpu.VMEM((N_PEERS, CHUNK, LANES), F32), pltpu.VMEM((ROWS, COLS), F32),
            rows, rows, pltpu.VMEM((2, LAYERS, DOWN_ROWS, COLS), F32),
            seven, seven, two, two, norm, norm, seven, seven, two, two,
        ],
        compiler_params=comm_params(3),
        name="update_rows",
    )(block, *arrays)


def keep_kernel(*refs):
    half = len(refs) // 2
    for src, dst in zip(refs[:half], refs[half:]):
        dst[...] = src[...]


def keep(arrays):
    return pl.pallas_call(
        keep_kernel,
        out_shape=[jax.ShapeDtypeStruct(a.shape, a.dtype) for a in arrays],
        in_specs=[in_vmem()] * len(arrays),
        out_specs=[in_vmem()] * len(arrays),
        compiler_params=plain_params(0),
        name="keep",
    )(*arrays)


SWAP = [(i, i ^ 1) for i in range(2 * RING * RING * RING)]


def swap_cores(array):
    return lax.ppermute(array, "fsdp", SWAP)


def rows_first(array):
    return jnp.transpose(array, (1, 0, 2))


def local_step(x_saved, grad_out, x_next, w_up, w_down, gacc_up, gacc_down, master_up, master_down, mom1_up, mom1_down, mom2_up, mom2_down):
    core = jnp.reshape(lax.rem(lax.axis_index("fsdp"), 2), (1,))
    x_tokens = x_saved.reshape(LAYERS, -1, WIDTH)
    grad_cur = grad_out.reshape(-1, WIDTH)
    operands = []
    for layer_idx in range(LAYERS - 1, -1, -1):
        x_in = x_tokens[layer_idx]
        pre_act = jnp.dot(x_in, w_up[layer_idx], preferred_element_type=F32)
        hidden_act, gelu_vjp = jax.vjp(gelu_fn, pre_act)
        d_act = lax.dot_general(grad_cur, w_down[layer_idx], (((1,), (1,)), ((), ())), preferred_element_type=F32)
        d_pre = gelu_vjp(d_act)[0].astype(BF16)
        operands.append((x_in, d_pre, hidden_act.astype(BF16), grad_cur))
        if layer_idx > 0:
            grad_cur = (grad_cur.astype(F32) + lax.dot_general(d_pre, w_up[layer_idx], (((1,), (1,)), ((), ())), preferred_element_type=F32)).astype(BF16)
    x_last, d_last, a_last, g_last = operands[0]
    sums = grad_sum(core, x_last, swap_cores(x_last), d_last, swap_cores(d_last), None)
    sums = grad_sum(core, a_last, swap_cores(a_last), g_last, swap_cores(g_last), sums)
    block = reduce_blocks(sums.reshape(RING, RING, RING, PAIR_ROWS, COLS), *operands[1])

    new_block, *state = update_rows(
        block, rows_first(gacc_up), gacc_down, rows_first(master_up), master_down,
        rows_first(mom1_up), mom1_down, rows_first(mom2_up), mom2_down,
    )
    weights = gather_blocks(new_block).reshape(2, RING * RING, RING, 2 * LAYERS, BLOCK, COLS)
    master_up, master_down, mom1_up, mom1_down, mom2_up, mom2_down = keep(state)

    hidden = x_next.reshape(-1, WIDTH)
    for layer_idx in range(LAYERS):
        hidden = forward_layer(hidden, weights, layer_idx)
    return (hidden.reshape(x_next.shape), rows_first(master_up), master_down, rows_first(mom1_up), mom1_down, rows_first(mom2_up), mom2_down)


def solution(mesh):
    rows_spec = P(None, "fsdp")
    return jax.shard_map(local_step, mesh=mesh, in_specs=(rows_spec, P("fsdp"), P("fsdp"), P(), P(), rows_spec, rows_spec, rows_spec, rows_spec, rows_spec, rows_spec, rows_spec, rows_spec), out_specs=(P("fsdp"), rows_spec, rows_spec, rows_spec, rows_spec, rows_spec, rows_spec), check_vma=False)
```

time: 1580 us -> 505 us (0.32)
  waiting for transfers between devices: 1140 us -> 0.01 us
  Pallas kernels: 0 us -> 437 us
  matrix products: 157 us -> 61.8 us
  starting transfers between devices: 80.8 us -> 1.02 us
  blocking collectives: 79.3 us -> 0 us
  local copies, waits for them, and re-layouts: 53.6 us -> 2.03 us
  other arithmetic: 36.5 us -> 0 us
    all_to_all x4 -> x0, waiting for transfers between devices: 836 us -> none  [reduce_rows(): received = lax.all_to_all(part_grad, 'fsdp', 0, 0, tiled=True)]
    pallas_call x0 -> x10, Pallas kernels: none -> 437 us  [the longest x1 222 us: reduce_blocks(): pl.pallas_call(reduce_kernel, out_shape=[jax.ShapeDtypeStruct((ROWS, COLS...]
    all_gather x4 -> x0, waiting for transfers between devices: 307 us -> none  [the longest x2 195 us: local_step(): w_layer_up = lax.all_gather(up_shard[layer_idx], 'fsdp', axis=0, tiled=True)]
    dot_general x10 -> x5, matrix products: 157 us -> 61.8 us  [the longest x2 28.1 us: local_step(): lax.dot_general(grad_cur, w_down[layer_idx], (((1,), (1,)), ((), ())), pr...]
    all_to_all x4 -> x0, starting transfers between devices: 80.5 us -> none  [reduce_rows(): received = lax.all_to_all(part_grad, 'fsdp', 0, 0, tiled=True)]
    psum x1 -> x0, blocking collectives: 79.3 us -> none  [backward_update(): lax.psum(local_sq, 'fsdp')]
    all_to_all x2 -> x0, local copies, waits for them, and re-layouts: 47.9 us -> none  [reduce_rows(): received = lax.all_to_all(part_grad, 'fsdp', 0, 0, tiled=True)]
    reduce_sum x6 -> x0, other arithmetic: 32.2 us -> none  [the longest x4 30.7 us: reduce_rows(): jnp.sum(received.reshape(n_dev, -1, part_grad.shape[1]), axis=0, dtype=jn...]
  transfers between devices with their start and end apart: 8 -> 4, of which waited for: 8 -> 0; matrix products, arithmetic and copies ran while one was open for 8% -> 8% of each run, Pallas kernels for 0% -> 3%
where the time goes in v1:
time: 505 us; the launch traced here: 503 us
  Pallas kernels  437 us (87%)
  matrix products  61.8 us (12%)
    pallas_call x1, Pallas kernels, reduce_blocks(): pl.pallas_call(reduce_kernel, out_shape=[jax.ShapeDtypeStruct((ROWS, COLS...  222 us
    pallas_call x1, Pallas kernels, gather_blocks(): pl.pallas_call(gather_kernel, out_shape=jax.ShapeDtypeStruct((2, RING, RI...  113 us
    pallas_call x1, Pallas kernels, update_rows(): pl.pallas_call(update_kernel, out_shape=[jax.ShapeDtypeStruct((ROWS, COLS...  29.7 us
    dot_general x2, matrix products, local_step(): lax.dot_general(grad_cur, w_down[layer_idx], (((1,), (1,)), ((), ())), pr...  28.1 us
    pallas_call x2, Pallas kernels, grad_sum(): pl.pallas_call(grad_kernel, out_shape=jax.ShapeDtypeStruct((zy, RING, 2,...  26.8 us
    dot_general x2, matrix products, local_step(): pre_act = jnp.dot(x_in, w_up[layer_idx], preferred_element_type=F32)  22.4 us
    pallas_call x2, Pallas kernels, forward_layer(): pl.pallas_call(up_kernel, out_shape=jax.ShapeDtypeStruct((tokens, FF), BF...  21.8 us
    pallas_call x2, Pallas kernels, forward_layer(): pl.pallas_call(down_kernel, out_shape=jax.ShapeDtypeStruct((tokens, WIDTH...  21 us
  transfers between devices with their start and end apart: 4, of which 0 were waited for; matrix products, arithmetic and copies ran while one was open for 8% of the time, Pallas kernels for 3%

profile of v1, /device:TPU:0, one launch (start us, length us, event | category | flops | bytes accessed | tf_op | source)
XLA Modules:
  0.0 502.9 jit_solution(4650015488049311755)
XLA Ops:
  0.6 10.7 %multiply_convert_fusion.1 = (bf16[384,5120]{1,0:T(8,128)(2,1)}, f32[384,5120]{1,0:T(8,128)S(1)}) fusion(bf16[2,1280,5120]{2,1,0:T(8,128)(2,1)} %param.16, bf16[2,1,384,1280]{3,2,1,0:T(8,128)(2,1)} %param.13), kind=kOutput, calls=%fused_computation.34 | convolution fusion | flops 5050859520 | bytes 25886720 | tf_op jit(solution)/shard_map/dot_general | solution.py:803
  11.4 0.0 copy-start.1
  11.4 13.4 %fusion.21.right = bf16[384,5120]{1,0:T(8,128)(2,1)} fusion(f32[384,5120]{1,0:T(8,128)S(1)} %get-tuple-element.38, bf16[2,5120,1280]{2,1,0:T(8,128)(2,1)} %param.17, bf16[1,384,1280]{2,1,0:T(8,128)(2,1)} %param.14), kind=kOutput, calls=%fused_computation.25 | convolution fusion | flops 5072486400 | bytes 25886720 | tf_op jit(solution)/shard_map/dot_general | solution.py:805
  24.8 0.0 collective-permute-start.3
  24.8 0.0 copy-done.1
  24.8 1.1 slice_bitcast_fusion
  25.9 0.0 copy-start
  25.9 0.5 collective-permute-start.2
  26.4 0.0 collective-permute-start
  26.4 0.5 collective-permute-start.1
  26.9 11.6 %multiply_convert_fusion = (bf16[384,5120]{1,0:T(8,128)(2,1)}, f32[384,5120]{1,0:T(8,128)}) fusion(bf16[2,1280,5120]{2,1,0:T(8,128)(2,1)} %param.16, bf16[2,1,384,1280]{3,2,1,0:T(8,128)(2,1)S(1)} %copy-done.1), kind=kOutput, calls=%fused_computation.33 | convolution fusion | flops 5050859520 | bytes 25886720 | tf_op jit(solution)/shard_map/dot_general | solution.py:803
  38.5 0.0 copy-done
  38.5 11.3 %fusion.36.g_own = bf16[384,1280]{1,0:T(8,128)(2,1)S(1)} fusion(bf16[384,5120]{1,0:T(8,128)(2,1)} %fusion.21.right, bf16[2,1280,5120]{2,1,0:T(8,128)(2,1)} %param.16, bf16[1,384,1280]{2,1,0:T(8,128)(2,1)} %param.14), kind=kOutput, calls=%fused_computation.36 | convolution fusion | flops 5034639360 | bytes 19005440 | tf_op jit(solution)/shard_map/dot_general | solution.py:809
  49.9 0.0 copy-start.2
  49.9 14.6 %fusion.28.d_own = bf16[384,5120]{1,0:T(8,128)(2,1)} fusion(f32[384,5120]{1,0:T(8,128)} %get-tuple-element.40, bf16[384,1280]{1,0:T(8,128)(2,1)S(1)} %fusion.36.g_own, bf16[2,5120,1280]{2,1,0:T(8,128)(2,1)} %param.17), kind=kOutput, calls=%fused_computation.32 | convolution fusion | flops 5072486400 | bytes 25886720 | tf_op jit(solution)/shard_map/dot_general | solution.py:805
  64.5 0.0 copy-done.2
  64.5 0.0 collective-permute-done.2.left_pair
  64.5 0.0 copy-start.3
  64.6 0.9 copy-done.3
  65.5 0.0 collective-permute-done.3.right_pair
  65.5 12.6 %grad_up.1.refs_0_ = f32[16,4,2,80,640]{4,3,2,1,0:T(8,128)} custom-call(s32[1]{0:T(128)} %bitcast.1.core_ref, bf16[384,1280]{1,0:T(8,128)(2,1)} %copy-done, bf16[384,1280]{1,0:T(8,128)(2,1)} %copy-done.3, bf16[384,5120]{1,0:T(8,128)(2,1)} %fusion.21.right, bf16[384,5120]{1,0:T(8,128)(2,1)} %collective-permute-done.3.right_pair), custom_call_target="tpu_custom_call" | custom-call | flops 5033164800 | bytes 17000000 | tf_op jit(solution)/shard_map/grad_up/pallas_call | solution.py:525
  78.1 0.0 collective-permute-done.1.right_pair
  78.1 0.0 collective-permute-done.left_pair
  78.1 14.2 %grad_down.1 = f32[16,4,2,80,640]{4,3,2,1,0:T(8,128)} custom-call(s32[1]{0:T(128)} %bitcast.1.core_ref, bf16[384,5120]{1,0:T(8,128)(2,1)} %get-tuple-element.37.left, bf16[384,5120]{1,0:T(8,128)(2,1)} %collective-permute-done.left_pair, bf16[384,1280]{1,0:T(8,128)(2,1)} %bitcast.4.right, ...), custom_call_target="tpu_custom_call", output_to_operand_aliasing={{}: (5, {})} | custom-call | flops 5033164800 | bytes 17000000 | tf_op jit(solution)/shard_map/grad_down/pallas_call | solution.py:525
  92.3 222.3 %torus_reduce.1 = (f32[320,640]{1,0:T(8,128)}, f32[4,4,4,160,640]{4,3,2,1,0:T(8,128)}, bf16[384,1280]{1,0:T(8,128)(2,1)}, bf16[384,2560]{1,0:T(8,128)(2,1)}, bf1...) custom-call(f32[4,4,4,160,640]{4,3,2,1,0:T(8,128)} %bitcast.58, bf16[384,1280]{1,0:T(8,128)(2,1)} %get-tuple-element.35.x_own, ...), custom_call_target="tpu_custom_call" | custom-call | tf_op jit(solution)/shard_map/torus_reduce/pallas_call | solution.py:365
  314.6 29.7 %update_rows.1 = (bf16[320,640]{1,0:T(8,128)(2,1)}, f32[10,2,5120]{2,1,0:T(2,128)}, f32[2,40,1280]{2,1,0:T(8,128)}, f32[10,2,5120]{2,1,0:T(2,128)}, f32[2,40,128...) custom-call(f32[320,640]{1,0:T(8,128)} %get-tuple-element.21.block, f32[10,2,5120]{2,1,0:T(2,128)} %bitcast.62, ...), custom_call_target="tpu_custom_call" | custom-call | tf_op jit(solution)/shard_map/update_rows/pallas_call | solution.py:752
  344.3 112.8 %torus_gather.1 = bf16[2,4,4,4,320,640]{5,4,3,2,1,0:T(8,128)(2,1)} custom-call(bf16[320,640]{1,0:T(8,128)(2,1)} %get-tuple-element.22.block_ref), custom_call_target="tpu_custom_call" | custom-call | tf_op jit(solution)/shard_map/torus_gather/pallas_call | solution.py:489
  457.1 11.0 %forward_up.2.act = bf16[384,5120]{1,0:T(8,128)(2,1)} custom-call(bf16[384,1280]{1,0:T(8,128)(2,1)} %bitcast.59, bf16[2,16,4,4,80,640]{5,4,3,2,1,0:T(8,128)(2,1)} %bitcast.54), custom_call_target="tpu_custom_call" | custom-call | tf_op jit(solution)/shard_map/forward_up/pallas_call | solution.py:568
  468.1 10.5 %forward_down.2.hidden = bf16[384,1280]{1,0:T(8,128)(2,1)} custom-call(bf16[384,5120]{1,0:T(8,128)(2,1)} %forward_up.2.act, bf16[2,16,4,4,80,640]{5,4,3,2,1,0:T(8,128)(2,1)} %bitcast.55, bf16[384,1280]{1,0:T(8,128)(2,1)} %bitcast.60), custom_call_target="tpu_custom_call" | custom-call | tf_op jit(solution)/shard_map/forward_down/pallas_call | solution.py:580
  478.6 10.8 %forward_up.3.act = bf16[384,5120]{1,0:T(8,128)(2,1)} custom-call(bf16[384,1280]{1,0:T(8,128)(2,1)} %forward_down.2.hidden, bf16[2,16,4,4,80,640]{5,4,3,2,1,0:T(8,128)(2,1)} %bitcast.56), custom_call_target="tpu_custom_call" | custom-call | tf_op jit(solution)/shard_map/forward_up/pallas_call | solution.py:568
  489.4 10.5 %forward_down.3 = bf16[384,1280]{1,0:T(8,128)(2,1)} custom-call(bf16[384,5120]{1,0:T(8,128)(2,1)} %forward_up.3.act, bf16[2,16,4,4,80,640]{5,4,3,2,1,0:T(8,128)(2,1)} %bitcast.57, bf16[384,1280]{1,0:T(8,128)(2,1)} %forward_down.2.hidden), custom_call_target="tpu_custom_call" | custom-call | tf_op jit(solution)/shard_map/forward_down/pallas_call | solution.py:580
  499.8 3.1 keep.1
Async XLA Ops:
  11.4 13.4 %copy-start.1 = (bf16[2,1,384,1280]{3,2,1,0:T(8,128)(2,1)S(1)}, bf16[2,1,384,1280]{3,2,1,0:T(8,128)(2,1)}, u32[]{:S(2)}) copy-start(bf16[2,1,384,1280]{3,2,1,0:T(8,128)(2,1)} %param.13) | copy-start | bytes 5898244
  24.8 40.7 %collective-permute-start.3 = (bf16[384,5120]{1,0:T(8,128)(2,1)}, bf16[384,5120]{1,0:T(8,128)(2,1)}, u32[]{:S(2)}, u32[]{:S(2)}) collective-permute-start(bf16[384,5120]{1,0:T(8,128)(2,1)} %fusion.21.right), channel_id=1, source_target_pairs={{0,1},{1,0},{2,3},{3,2},{4,5},{5,4},{6,7},{7,6},{8,9},{9,8},{10,11... | collective-permute-start | bytes 11796488 | tf_op jit(solution)/shard_map/ppermute | solution.py:789
  25.9 12.7 %copy-start = (bf16[384,1280]{1,0:T(8,128)(2,1)}, bf16[384,1280]{1,0:T(8,128)(2,1)S(1)}, u32[]{:S(2)}) copy-start(bf16[384,1280]{1,0:T(8,128)(2,1)S(1)} %get-tuple-element.36.left) | copy-start | bytes 2949124
  25.9 38.7 %collective-permute-start.2 = (bf16[384,1280]{1,0:T(8,128)(2,1)S(1)}, bf16[384,1280]{1,0:T(8,128)(2,1)S(1)}, u32[]{:S(2)}, u32[]{:S(2)}) collective-permute-start(bf16[384,1280]{1,0:T(8,128)(2,1)S(1)} %get-tuple-element.36.left), channel_id=1, source_target_pairs={{0,1},{1,0},{2,3},{3,2},{4,5},{5,4},{6,7},{7,6},{8,9},{9,8},{10,11... | collective-permute-start | bytes 2949128 | tf_op jit(solution)/shard_map/ppermute | solution.py:789
  26.4 51.7 %collective-permute-start = (bf16[384,5120]{1,0:T(8,128)(2,1)}, bf16[384,5120]{1,0:T(8,128)(2,1)}, u32[]{:S(2)}, u32[]{:S(2)}) collective-permute-start(bf16[384,5120]{1,0:T(8,128)(2,1)} %get-tuple-element.37.left), channel_id=1, source_target_pairs={{0,1},{1,0},{2,3},{3,2},{4,5},{5,4},{6,7},{7,6},{8,9},{9,8},{10,11... | collective-permute-start | bytes 11796488 | tf_op jit(solution)/shard_map/ppermute | solution.py:789
  26.4 51.7 %collective-permute-start.1 = (bf16[384,1280]{1,0:T(8,128)(2,1)}, bf16[384,1280]{1,0:T(8,128)(2,1)}, u32[]{:S(2)}, u32[]{:S(2)}) collective-permute-start(bf16[384,1280]{1,0:T(8,128)(2,1)} %bitcast.4.right), channel_id=1, source_target_pairs={{0,1},{1,0},{2,3},{3,2},{4,5},{5,4},{6,7},{7,6},{8,9},{9,8},{10,11... | collective-permute-start | bytes 2949128 | tf_op jit(solution)/shard_map/ppermute | solution.py:789
  49.9 14.6 %copy-start.2 = (bf16[384,1280]{1,0:T(8,128)(2,1)}, bf16[384,1280]{1,0:T(8,128)(2,1)S(1)}, u32[]{:S(2)}) copy-start(bf16[384,1280]{1,0:T(8,128)(2,1)S(1)} %fusion.36.g_own) | copy-start | bytes 2949124
  64.5 1.0 copy-start.3

commit v2 on v1

--- a/solution.py
+++ b/solution.py
@@ -382,119 +382,180 @@
     )(s_last, x_first, d_first, a_first, g_first)[0]
 
 
-GATHER_LEN = [BATCH_LEN[0][f] + BATCH_LEN[1][f] for f in FLOWS]
-GATHER_START = [sum(GATHER_LEN[:f]) for f in FLOWS]
-
-
-def gather_kernel(block_ref, all_ref, own_sem, send1, got1, send2, got2, send3, got3, pair_send, pair_got):
+N_MATRICES = 2 * LAYERS
+MATRIX_BASE = [base for layer in range(LAYERS) for base in (up_base(layer), down_base(layer))]
+SHORT = (2, 1, 0, 2)
+MATRIX_LEN = [[CHUNK if f // 2 == SHORT[q] else 2 * CHUNK for f in FLOWS] for q in range(N_MATRICES)]
+MATRIX_START = [[MATRIX_BASE[q] + sum(MATRIX_LEN[q][:f]) for f in FLOWS] for q in range(N_MATRICES)]
+
+
+def gather_kernel(
+    block_ref, x_ref, all_ref, hidden_ref, act_ref,
+    total, weight, own_sem, load_sem, send1, got1, send2, got2, send3, got3, pair_send, pair_got,
+):
     core, pos = my_place()
     partner = device_at(pos, 1 - core)
     entry_barrier([partner] + all_neighbors(pos, core))
     target = [[neighbor(pos, core, dim, flow_sign(f)) for dim in flow_dims(f)] for f in FLOWS]
-
-    def flow_rows(flow):
-        return pl.ds(GATHER_START[flow] * CHUNK, GATHER_LEN[flow] * CHUNK)
+    pieces = [(q, f) for q in range(N_MATRICES) for f in FLOWS]
+
+    def rows_of(q, flow):
+        return pl.ds(MATRIX_START[q][flow], MATRIX_LEN[q][flow])
 
     def back(flow, phase, steps):
         at = pos[flow_dims(flow)[phase]]
         return lax.rem(at + RING - flow_sign(flow) * steps, RING)
 
-    def place(flow, first, second, third):
-        index = [None] * 3
-        for dim, at in zip(flow_dims(flow), (first, second, third)):
-            index[dim] = at
-        return all_ref.at[(core, *index, flow_rows(flow), slice(None))]
-
-    def copy1(flow, step):
-        ref = place(flow, back(flow, 0, step), back(flow, 1, 0), back(flow, 2, 0))
-        if step == 0:
-            return remote(block_ref.at[flow_rows(flow)], ref, send1.at[flow, step], got1.at[flow, step], target[flow][0])
-        return remote(ref, ref, send1.at[flow, step], got1.at[flow, step], target[flow][0])
-
-    def wait1(flow, step):
-        ref = place(flow, back(flow, 0, step + 1), back(flow, 1, 0), back(flow, 2, 0))
-        remote(ref, ref, send1.at[flow, step], got1.at[flow, step], target[flow][0]).wait_recv()
-
-    def copy2(flow, step, u, off=0):
-        ref = place(flow, back(flow, 0, u), back(flow, 1, step + off), back(flow, 2, 0))
-        if step == 0 and u == 0 and off == 0:
-            return remote(block_ref.at[flow_rows(flow)], ref, send2.at[flow, step, u], got2.at[flow, step, u], target[flow][1])
-        return remote(ref, ref, send2.at[flow, step, u], got2.at[flow, step, u], target[flow][1])
-
-    def copy3(flow, step, v, off=0):
-        ref = place(flow, slice(None), back(flow, 1, v), back(flow, 2, step + off))
-        return remote(ref, ref, send3.at[flow, step, v], got3.at[flow, step, v], target[flow][2])
-
-    def pair_copy(flow, w, v):
-        ref = place(flow, slice(None), back(flow, 1, v), back(flow, 2, w))
-        return remote(ref, ref, pair_send.at[flow, w, v], pair_got.at[flow, w, v], partner)
-
-    def pair_wait(flow, w, v):
-        index = [None] * 3
-        for dim, at in zip(flow_dims(flow), (slice(None), back(flow, 1, v), back(flow, 2, w))):
-            index[dim] = at
-        ref = all_ref.at[(1 - core, *index, flow_rows(flow), slice(None))]
-        remote(ref, ref, pair_send.at[flow, w, v], pair_got.at[flow, w, v], partner).wait_recv()
-
-    flows = FLOWS
+    def place(which, q, flow, *at):
+        index = [slice(None)] * 3
+        for phase, steps in enumerate(at):
+            if steps is not None:
+                index[flow_dims(flow)[phase]] = back(flow, phase, steps)
+        return all_ref.at[(which, *index, rows_of(q, flow), slice(None))]
+
+    def copy1(q, flow, step, off=0):
+        dst = place(core, q, flow, step + off, 0, 0)
+        src = dst if off or step else block_ref.at[rows_of(q, flow)]
+        return remote(src, dst, send1.at[q, flow, step], got1.at[q, flow, step], target[flow][0])
+
+    def copy2(q, flow, step, off=0):
+        ref = place(core, q, flow, None, step + off, 0)
+        return remote(ref, ref, send2.at[q, flow, step], got2.at[q, flow, step], target[flow][1])
+
+    def copy3(q, flow, step, v, off=0):
+        ref = place(core, q, flow, None, v, step + off)
+        return remote(ref, ref, send3.at[q, flow, step, v], got3.at[q, flow, step, v], target[flow][2])
+
+    def pair_copy(q, flow, w, which=core):
+        ref = place(which, q, flow, None, None, w)
+        return remote(ref, ref, pair_send.at[q, flow, w], pair_got.at[q, flow, w], partner)
+
     local = pltpu.make_async_copy(block_ref, all_ref.at[core, pos[0], pos[1], pos[2]], own_sem)
     local.start()
-    for f in flows:
-        copy1(f, 0).start()
-    for f in flows:
-        copy2(f, 0, 0).start()
+    for q, f in pieces:
+        copy1(q, f, 0).start()
     local.wait()
     for step in range(STEPS):
-        for f in flows:
-            wait1(f, step)
+        for q, f in pieces:
+            copy1(q, f, step, 1).wait_recv()
             if step < STEPS - 1:
-                copy1(f, step + 1).start()
-            copy2(f, 0, step + 1).start()
-    for f in flows:
-        copy3(f, 0, 0).start()
-        pair_copy(f, 0, 0).start()
+                copy1(q, f, step + 1).start()
+            else:
+                copy2(q, f, 0).start()
+    for q, f in pieces:
+        copy3(q, f, 0, 0).start()
     for step in range(STEPS):
-        for u in range(RING):
-            for f in flows:
-                copy2(f, step, u, 1).wait_recv()
-                if step < STEPS - 1:
-                    copy2(f, step + 1, u).start()
-                if u == RING - 1:
-                    copy3(f, 0, step + 1).start()
-                    pair_copy(f, 0, step + 1).start()
-    for step in range(STEPS):
-        for v in range(RING):
-            for f in flows:
-                copy3(f, step, v, 1).wait_recv()
-                if step < STEPS - 1:
-                    copy3(f, step + 1, v).start()
-                pair_copy(f, step + 1, v).start()
-    for w in range(RING):
-        for v in range(RING):
-            for f in flows:
-                pair_wait(f, w, v)
-    for f in flows:
+        for q, f in pieces:
+            copy2(q, f, step, 1).wait_recv()
+            if step < STEPS - 1:
+                copy2(q, f, step + 1).start()
+            copy3(q, f, 0, step + 1).start()
+    for q, f in pieces:
+        pair_copy(q, f, 0).start()
+
+    @pl.loop(0, STEPS - 1)
+    def _(step):
+        for q in range(N_MATRICES):
+            for v in range(RING):
+                for f in FLOWS:
+                    copy3(q, f, step, v, 1).wait_recv()
+                    copy3(q, f, step + 1, v).start()
+            for f in FLOWS:
+                pair_copy(q, f, step + 1).start()
+
+    def last_step(q):
+        for f in FLOWS:
+            for v in range(RING):
+                copy3(q, f, STEPS - 1, v, 1).wait_recv()
+            pair_copy(q, f, STEPS).start()
+
+    def have_pair(q):
+        for f in FLOWS:
+            for w in range(RING):
+                pair_copy(q, f, w, 1 - core).wait_recv()
+
+    def load(q, i):
+        rows = pl.ds(MATRIX_BASE[q], BLOCK)
+        if q % 2 == 0:
+            src = all_ref.at[lax.div(i, 2), :, :, pl.ds(lax.rem(i, 2) * 2, 2), rows]
+        else:
+            src = all_ref.at[:, i, :, :, rows]
+        slot = lax.rem(i, 2)
+        dst = weight.at[slot].reshape(src.shape)
+        return pltpu.make_async_copy(src, dst, load_sem.at[slot])
+
+    def product(q, i):
+        slot = lax.rem(i, 2)
+        cols = aligned_lanes(i * WIDTH, WIDTH)
+        if q % 2 == 0:
+            tiles = weight[slot].reshape(RING * RING, 2, BLOCK, COLS)
+            wide = jnp.concatenate([tiles[:, x].reshape(WIDTH, COLS) for x in range(2)], axis=1)
+            hidden = x_ref if q == 0 else hidden_ref
+            act_ref[:, cols] = gelu_fn(jnp.dot(hidden[...], wide, preferred_element_type=F32)).astype(BF16)
+        else:
+            tiles = weight[slot].reshape(2, WIDTH, COLS)
+            wide = jnp.concatenate([tiles[c] for c in range(2)], axis=1)
+            total[...] += jnp.dot(act_ref[:, cols], wide, preferred_element_type=F32)
+
+    last_step(0)
+    have_pair(0)
+    load(0, 0).start()
+    for q in range(N_MATRICES - 1):
+        if q % 2:
+            total[...] = x_ref[...].astype(F32)
+
+        @pl.loop(0, RING)
+        def _(i):
+            load(q, i).wait()
+
+            @pl.when(i < RING - 1)
+            def _():
+                load(q, i + 1).start()
+
+            @pl.when(i == RING - 1)
+            def _():
+                have_pair(q + 1)
+                if q + 1 < N_MATRICES - 1:
+                    load(q + 1, 0).start()
+
+            product(q, i)
+
+            @pl.when(i == 1)
+            def _():
+                last_step(q + 1)
+
+        if q % 2:
+            hidden_ref[...] = total[...].astype(BF16)
+    for q, f in pieces:
         for step in range(STEPS):
-            copy1(f, step).wait_send()
-            for u in range(RING):
-                copy2(f, step, u).wait_send()
-                copy3(f, step, u).wait_send()
+            copy1(q, f, step).wait_send()
+            copy2(q, f, step).wait_send()
+            for v in range(RING):
+                copy3(q, f, step, v).wait_send()
         for w in range(RING):
-            for v in range(RING):
-                pair_copy(f, w, v).wait_send()
-
-
-def gather_blocks(block):
-    one, four, pair = SEMS((N_FLOWS, STEPS)), SEMS((N_FLOWS, STEPS, RING)), SEMS((N_FLOWS, RING, RING))
+            pair_copy(q, f, w).wait_send()
+
+
+def gather_forward(block, x_next):
+    tokens = x_next.shape[0]
+    one, four = SEMS((N_MATRICES, N_FLOWS, STEPS)), SEMS((N_MATRICES, N_FLOWS, STEPS, RING))
+    pair = SEMS((N_MATRICES, N_FLOWS, RING))
     return pl.pallas_call(
         gather_kernel,
-        out_shape=jax.ShapeDtypeStruct((2, RING, RING, RING, ROWS, COLS), BF16),
-        in_specs=[in_vmem()],
-        out_specs=in_hbm(),
-        scratch_shapes=[SEMS, one, one, four, four, four, four, pair, pair],
+        out_shape=[
+            jax.ShapeDtypeStruct((2, RING, RING, RING, ROWS, COLS), BF16),
+            jax.ShapeDtypeStruct((tokens, WIDTH), BF16),
+            jax.ShapeDtypeStruct((tokens, FF), BF16),
+        ],
+        in_specs=[in_vmem(), in_vmem()],
+        out_specs=[in_hbm(), in_vmem(), in_vmem()],
+        scratch_shapes=[
+            pltpu.VMEM((tokens, WIDTH), F32), pltpu.VMEM((2, 2, RING, RING, BLOCK, COLS), BF16),
+            SEMS, SEMS((2,)), one, one, one, one, four, four, pair, pair,
+        ],
         compiler_params=comm_params(2),
-        name="torus_gather",
-    )(block)
+        name="torus_gather_forward",
+    )(block, x_next)
 
 
 def grad_kernel(core_ref, left, left_pair, right, right_pair, *refs):
@@ -542,12 +603,6 @@
     return jax.nn.gelu(pre_act, approximate=True)
 
 
-def up_kernel(hidden, weight, out):
-    wide = jnp.concatenate([weight[0, :, x, 0].reshape(WIDTH, COLS) for x in range(2)], axis=1)
-    pre_act = jnp.dot(hidden[...], wide, preferred_element_type=F32)
-    out[...] = gelu_fn(pre_act).astype(BF16)
-
-
 def down_kernel(act, weight, hidden, out, total):
     step = pl.program_id(0)
 
@@ -563,27 +618,15 @@
         out[...] = total[...].astype(BF16)
 
 
-def forward_layer(hidden, weights, layer):
+def last_product(act, weights, hidden):
     tokens = hidden.shape[0]
-    act = pl.pallas_call(
-        up_kernel,
-        out_shape=jax.ShapeDtypeStruct((tokens, FF), BF16),
-        grid=(2, 2),
-        in_specs=[
-            pl.BlockSpec((tokens, WIDTH), lambda c, x: (0, 0)),
-            pl.BlockSpec((1, 16, 2, 1, BLOCK, COLS), lambda c, x: (c, 0, x, 2 * (LAYERS - 1 - layer), 0, 0)),
-        ],
-        out_specs=pl.BlockSpec((tokens, 2 * COLS), lambda c, x: (0, c * 2 + x)),
-        compiler_params=plain_params(2),
-        name="forward_up",
-    )(hidden, weights)
     return pl.pallas_call(
         down_kernel,
         out_shape=jax.ShapeDtypeStruct((tokens, WIDTH), BF16),
-        grid=(4,),
+        grid=(RING,),
         in_specs=[
             pl.BlockSpec((tokens, WIDTH), lambda i: (0, i)),
-            pl.BlockSpec((2, 4, 4, 1, BLOCK, COLS), lambda i: (0, i, 0, 2 * (LAYERS - 1 - layer) + 1, 0, 0)),
+            pl.BlockSpec((2, RING, RING, 1, BLOCK, COLS), lambda i: (0, i, 0, 1, 0, 0)),
             pl.BlockSpec((tokens, WIDTH), lambda i: (0, 0)),
         ],
         out_specs=pl.BlockSpec((tokens, WIDTH), lambda i: (0, 0)),
@@ -816,12 +859,10 @@
         block, rows_first(gacc_up), gacc_down, rows_first(master_up), master_down,
         rows_first(mom1_up), mom1_down, rows_first(mom2_up), mom2_down,
     )
-    weights = gather_blocks(new_block).reshape(2, RING * RING, RING, 2 * LAYERS, BLOCK, COLS)
+    weights, hidden, act = gather_forward(new_block, x_next.reshape(-1, WIDTH))
+    weights = weights.reshape(2, RING * RING, RING, N_MATRICES, BLOCK, COLS)
+    hidden = last_product(act, weights, hidden)
     master_up, master_down, mom1_up, mom1_down, mom2_up, mom2_down = keep(state)
-
-    hidden = x_next.reshape(-1, WIDTH)
-    for layer_idx in range(LAYERS):
-        hidden = forward_layer(hidden, weights, layer_idx)
     return (hidden.reshape(x_next.shape), rows_first(master_up), master_down, rows_first(mom1_up), mom1_down, rows_first(mom2_up), mom2_down)
 
 

time: 505 us -> 499 us (0.988)
  Pallas kernels: 437 us -> 426 us
    pallas_call x5 -> x2, Pallas kernels: 156 us -> 144 us  [the longest x1 134 us: gather_forward(): pl.pallas_call(gather_kernel, out_shape=[jax.ShapeDtypeStruct((2, RING, R...]
where the time goes in v2:
time: 499 us; the launch traced here: 492 us
  Pallas kernels  426 us (85%)
  matrix products  62 us (12%)
    pallas_call x1, Pallas kernels, reduce_blocks(): pl.pallas_call(reduce_kernel, out_shape=[jax.ShapeDtypeStruct((ROWS, COLS...  222 us
    pallas_call x1, Pallas kernels, gather_forward(): pl.pallas_call(gather_kernel, out_shape=[jax.ShapeDtypeStruct((2, RING, R...  134 us
    pallas_call x1, Pallas kernels, update_rows(): pl.pallas_call(update_kernel, out_shape=[jax.ShapeDtypeStruct((ROWS, COLS...  29.6 us
    dot_general x2, matrix products, local_step(): lax.dot_general(grad_cur, w_down[layer_idx], (((1,), (1,)), ((), ())), pr...  28.1 us
    pallas_call x2, Pallas kernels, grad_sum(): pl.pallas_call(grad_kernel, out_shape=jax.ShapeDtypeStruct((zy, RING, 2,...  26.8 us
    dot_general x2, matrix products, local_step(): pre_act = jnp.dot(x_in, w_up[layer_idx], preferred_element_type=F32)  22.5 us
    dot_general x1, matrix products, local_step(): lax.dot_general(d_pre, w_up[layer_idx], (((1,), (1,)), ((), ())), preferr...  11.3 us
    pallas_call x1, Pallas kernels, last_product(): pl.pallas_call(down_kernel, out_shape=jax.ShapeDtypeStruct((tokens, WIDTH...  10.5 us
  transfers between devices with their start and end apart: 4, of which 0 were waited for; matrix products, arithmetic and copies ran while one was open for 8% of the time, Pallas kernels for 3%

profile of v2, /device:TPU:0, one launch (start us, length us, event | category | flops | bytes accessed | tf_op | source)
XLA Modules:
  0.0 492.5 jit_solution(16464537356628008894)
XLA Ops:
  0.6 10.8 %multiply_convert_fusion.1 = (bf16[384,5120]{1,0:T(8,128)(2,1)}, f32[384,5120]{1,0:T(8,128)S(1)}) fusion(bf16[2,1280,5120]{2,1,0:T(8,128)(2,1)} %param.16, bf16[2,1,384,1280]{3,2,1,0:T(8,128)(2,1)} %param.13), kind=kOutput, calls=%fused_computation.34 | convolution fusion | flops 5050859520 | bytes 25886720 | tf_op jit(solution)/shard_map/dot_general | solution.py:846
  11.5 0.0 copy-start.1
  11.5 13.4 %fusion.21.right = bf16[384,5120]{1,0:T(8,128)(2,1)} fusion(f32[384,5120]{1,0:T(8,128)S(1)} %get-tuple-element.44, bf16[2,5120,1280]{2,1,0:T(8,128)(2,1)} %param.17, bf16[1,384,1280]{2,1,0:T(8,128)(2,1)} %param.14), kind=kOutput, calls=%fused_computation.25 | convolution fusion | flops 5072486400 | bytes 25886720 | tf_op jit(solution)/shard_map/dot_general | solution.py:848
  24.9 0.0 collective-permute-start.3
  24.9 0.0 copy-done.1
  24.9 1.1 slice_bitcast_fusion
  26.0 0.0 copy-start
  26.0 0.5 collective-permute-start.2
  26.5 0.0 collective-permute-start
  26.5 0.7 collective-permute-start.1
  27.2 11.7 %multiply_convert_fusion = (bf16[384,5120]{1,0:T(8,128)(2,1)}, f32[384,5120]{1,0:T(8,128)}) fusion(bf16[2,1280,5120]{2,1,0:T(8,128)(2,1)} %param.16, bf16[2,1,384,1280]{3,2,1,0:T(8,128)(2,1)S(1)} %copy-done.1), kind=kOutput, calls=%fused_computation.33 | convolution fusion | flops 5050859520 | bytes 25886720 | tf_op jit(solution)/shard_map/dot_general | solution.py:846
  38.9 0.0 copy-done
  38.9 11.3 %fusion.36.g_own = bf16[384,1280]{1,0:T(8,128)(2,1)S(1)} fusion(bf16[384,5120]{1,0:T(8,128)(2,1)} %fusion.21.right, bf16[2,1280,5120]{2,1,0:T(8,128)(2,1)} %param.16, bf16[1,384,1280]{2,1,0:T(8,128)(2,1)} %param.14), kind=kOutput, calls=%fused_computation.36 | convolution fusion | flops 5034639360 | bytes 19005440 | tf_op jit(solution)/shard_map/dot_general | solution.py:852
  50.2 0.0 copy-start.2
  50.2 14.7 %fusion.28.d_own = bf16[384,5120]{1,0:T(8,128)(2,1)} fusion(f32[384,5120]{1,0:T(8,128)} %get-tuple-element.46, bf16[384,1280]{1,0:T(8,128)(2,1)S(1)} %fusion.36.g_own, bf16[2,5120,1280]{2,1,0:T(8,128)(2,1)} %param.17), kind=kOutput, calls=%fused_computation.32 | convolution fusion | flops 5072486400 | bytes 25886720 | tf_op jit(solution)/shard_map/dot_general | solution.py:848
  64.9 0.0 copy-done.2
  64.9 0.0 collective-permute-done.2.left_pair
  64.9 0.0 copy-start.3
  64.9 1.0 copy-done.3
  65.9 0.0 collective-permute-done.3.right_pair
  65.9 12.6 %grad_up.1.refs_0_ = f32[16,4,2,80,640]{4,3,2,1,0:T(8,128)} custom-call(s32[1]{0:T(128)} %bitcast.core_ref, bf16[384,1280]{1,0:T(8,128)(2,1)} %copy-done, bf16[384,1280]{1,0:T(8,128)(2,1)} %copy-done.3, bf16[384,5120]{1,0:T(8,128)(2,1)} %fusion.21.right, bf16[384,5120]{1,0:T(8,128)(2,1)} %collective-permute-done.3.right_pair), custom_call_target="tpu_custom_call" | custom-call | flops 5033164800 | bytes 17000000 | tf_op jit(solution)/shard_map/grad_up/pallas_call | solution.py:586
  78.4 0.0 collective-permute-done.1.right_pair
  78.4 0.0 collective-permute-done.left_pair
  78.5 14.2 %grad_down.1 = f32[16,4,2,80,640]{4,3,2,1,0:T(8,128)} custom-call(s32[1]{0:T(128)} %bitcast.core_ref, bf16[384,5120]{1,0:T(8,128)(2,1)} %get-tuple-element.43.left, bf16[384,5120]{1,0:T(8,128)(2,1)} %collective-permute-done.left_pair, bf16[384,1280]{1,0:T(8,128)(2,1)} %bitcast.3.right, ...), custom_call_target="tpu_custom_call", output_to_operand_aliasing={{}: (5, {})} | custom-call | flops 5033164800 | bytes 17000000 | tf_op jit(solution)/shard_map/grad_down/pallas_call | solution.py:586
  92.6 222.3 %torus_reduce.1 = (f32[320,640]{1,0:T(8,128)}, f32[4,4,4,160,640]{4,3,2,1,0:T(8,128)}, bf16[384,1280]{1,0:T(8,128)(2,1)}, bf16[384,2560]{1,0:T(8,128)(2,1)}, bf1...) custom-call(f32[4,4,4,160,640]{4,3,2,1,0:T(8,128)} %bitcast.54, bf16[384,1280]{1,0:T(8,128)(2,1)} %get-tuple-element.41.x_own, ...), custom_call_target="tpu_custom_call" | custom-call | tf_op jit(solution)/shard_map/torus_reduce/pallas_call | solution.py:365
  315.0 29.6 %update_rows.1 = (bf16[320,640]{1,0:T(8,128)(2,1)}, f32[10,2,5120]{2,1,0:T(2,128)}, f32[2,40,1280]{2,1,0:T(8,128)}, f32[10,2,5120]{2,1,0:T(2,128)}, f32[2,40,128...) custom-call(f32[320,640]{1,0:T(8,128)} %get-tuple-element.24.block, f32[10,2,5120]{2,1,0:T(2,128)} %bitcast.58, ...), custom_call_target="tpu_custom_call" | custom-call | tf_op jit(solution)/shard_map/update_rows/pallas_call | solution.py:795
  344.6 133.9 %torus_gather_forward.1 = (bf16[2,4,4,4,320,640]{5,4,3,2,1,0:T(8,128)(2,1)}, bf16[384,1280]{1,0:T(8,128)(2,1)}, bf16[384,5120]{1,0:T(8,128)(2,1)}) custom-call(bf16[320,640]{1,0:T(8,128)(2,1)} %get-tuple-element.25.block_ref, bf16[384,1280]{1,0:T(8,128)(2,1)} %bitcast.57), custom_call_target="tpu_custom_call" | custom-call | tf_op jit(solution)/shard_map/torus_gather_forward/pallas_call | solution.py:543
  478.5 10.5 %forward_down.1 = bf16[384,1280]{1,0:T(8,128)(2,1)} custom-call(bf16[384,5120]{1,0:T(8,128)(2,1)} %get-tuple-element.26.act, bf16[2,16,4,4,80,640]{5,4,3,2,1,0:T(8,128)(2,1)} %bitcast.55, bf16[384,1280]{1,0:T(8,128)(2,1)} %get-tuple-element.28.hidden), custom_call_target="tpu_custom_call" | custom-call | tf_op jit(solution)/shard_map/forward_down/pallas_call | solution.py:623
  489.0 3.1 keep.1
Async XLA Ops:
  11.5 13.4 %copy-start.1 = (bf16[2,1,384,1280]{3,2,1,0:T(8,128)(2,1)S(1)}, bf16[2,1,384,1280]{3,2,1,0:T(8,128)(2,1)}, u32[]{:S(2)}) copy-start(bf16[2,1,384,1280]{3,2,1,0:T(8,128)(2,1)} %param.13) | copy-start | bytes 5898244
  24.9 41.0 %collective-permute-start.3 = (bf16[384,5120]{1,0:T(8,128)(2,1)}, bf16[384,5120]{1,0:T(8,128)(2,1)}, u32[]{:S(2)}, u32[]{:S(2)}) collective-permute-start(bf16[384,5120]{1,0:T(8,128)(2,1)} %fusion.21.right), channel_id=1, source_target_pairs={{0,1},{1,0},{2,3},{3,2},{4,5},{5,4},{6,7},{7,6},{8,9},{9,8},{10,11... | collective-permute-start | bytes 11796488 | tf_op jit(solution)/shard_map/ppermute | solution.py:832
  26.0 12.9 %copy-start = (bf16[384,1280]{1,0:T(8,128)(2,1)}, bf16[384,1280]{1,0:T(8,128)(2,1)S(1)}, u32[]{:S(2)}) copy-start(bf16[384,1280]{1,0:T(8,128)(2,1)S(1)} %get-tuple-element.42.left) | copy-start | bytes 2949124
  26.0 38.9 %collective-permute-start.2 = (bf16[384,1280]{1,0:T(8,128)(2,1)S(1)}, bf16[384,1280]{1,0:T(8,128)(2,1)S(1)}, u32[]{:S(2)}, u32[]{:S(2)}) collective-permute-start(bf16[384,1280]{1,0:T(8,128)(2,1)S(1)} %get-tuple-element.42.left), channel_id=1, source_target_pairs={{0,1},{1,0},{2,3},{3,2},{4,5},{5,4},{6,7},{7,6},{8,9},{9,8},{10,11... | collective-permute-start | bytes 2949128 | tf_op jit(solution)/shard_map/ppermute | solution.py:832
  26.5 51.9 %collective-permute-start = (bf16[384,5120]{1,0:T(8,128)(2,1)}, bf16[384,5120]{1,0:T(8,128)(2,1)}, u32[]{:S(2)}, u32[]{:S(2)}) collective-permute-start(bf16[384,5120]{1,0:T(8,128)(2,1)} %get-tuple-element.43.left), channel_id=1, source_target_pairs={{0,1},{1,0},{2,3},{3,2},{4,5},{5,4},{6,7},{7,6},{8,9},{9,8},{10,11... | collective-permute-start | bytes 11796488 | tf_op jit(solution)/shard_map/ppermute | solution.py:832
  26.5 51.9 %collective-permute-start.1 = (bf16[384,1280]{1,0:T(8,128)(2,1)}, bf16[384,1280]{1,0:T(8,128)(2,1)}, u32[]{:S(2)}, u32[]{:S(2)}) collective-permute-start(bf16[384,1280]{1,0:T(8,128)(2,1)} %bitcast.3.right), channel_id=1, source_target_pairs={{0,1},{1,0},{2,3},{3,2},{4,5},{5,4},{6,7},{7,6},{8,9},{9,8},{10,11... | collective-permute-start | bytes 2949128 | tf_op jit(solution)/shard_map/ppermute | solution.py:832
  50.2 14.7 %copy-start.2 = (bf16[384,1280]{1,0:T(8,128)(2,1)}, bf16[384,1280]{1,0:T(8,128)(2,1)S(1)}, u32[]{:S(2)}) copy-start(bf16[384,1280]{1,0:T(8,128)(2,1)S(1)} %fusion.36.g_own) | copy-start | bytes 2949124
  64.9 1.0 copy-start.3

commit v3 on v2

--- a/solution.py
+++ b/solution.py
@@ -389,6 +389,19 @@
 MATRIX_START = [[MATRIX_BASE[q] + sum(MATRIX_LEN[q][:f]) for f in FLOWS] for q in range(N_MATRICES)]
 
 
+LINK_ORDER = ((0, 0), (1, 0), (0, 1), (1, 1), (0, 2), (2, 0), (1, 2), (2, 1), (3, 0), (2, 2), (3, 1), (3, 2))
+AHEAD = 2
+
+
+def before(at):
+    q, step = LINK_ORDER[at]
+    return LINK_ORDER.index((q, step - 1)) if step else -1
+
+
+GROUP_EVENTS = ((range(0, 6), (0,)), (range(6, 7), ()), (range(7, 8), (1,)), (range(8, 9), ()), (range(9, 11), (2,)), (range(11, 12), ()))
+LAST_EVENTS = ()
+
+
 def gather_kernel(
     block_ref, x_ref, all_ref, hidden_ref, act_ref,
     total, weight, own_sem, load_sem, send1, got1, send2, got2, send3, got3, pair_send, pair_got,
@@ -422,9 +435,9 @@
         ref = place(core, q, flow, None, step + off, 0)
         return remote(ref, ref, send2.at[q, flow, step], got2.at[q, flow, step], target[flow][1])
 
-    def copy3(q, flow, step, v, off=0):
-        ref = place(core, q, flow, None, v, step + off)
-        return remote(ref, ref, send3.at[q, flow, step, v], got3.at[q, flow, step, v], target[flow][2])
+    def copy3(q, flow, step, off=0):
+        ref = place(core, q, flow, None, None, step + off)
+        return remote(ref, ref, send3.at[q, flow, step], got3.at[q, flow, step], target[flow][2])
 
     def pair_copy(q, flow, w, which=core):
         ref = place(which, q, flow, None, None, w)
@@ -442,103 +455,99 @@
                 copy1(q, f, step + 1).start()
             else:
                 copy2(q, f, 0).start()
-    for q, f in pieces:
-        copy3(q, f, 0, 0).start()
     for step in range(STEPS):
         for q, f in pieces:
             copy2(q, f, step, 1).wait_recv()
             if step < STEPS - 1:
                 copy2(q, f, step + 1).start()
-            copy3(q, f, 0, step + 1).start()
+            elif (q, 0) in LINK_ORDER[:AHEAD]:
+                copy3(q, f, 0).start()
     for q, f in pieces:
         pair_copy(q, f, 0).start()
 
-    @pl.loop(0, STEPS - 1)
-    def _(step):
-        for q in range(N_MATRICES):
-            for v in range(RING):
-                for f in FLOWS:
-                    copy3(q, f, step, v, 1).wait_recv()
-                    copy3(q, f, step + 1, v).start()
-            for f in FLOWS:
-                pair_copy(q, f, step + 1).start()
-
-    def last_step(q):
+    def arrive(k):
+        q, step = LINK_ORDER[k]
+        due = [at for at in (k + AHEAD - 1, k + AHEAD) if at < len(LINK_ORDER) and max(at - AHEAD, before(at)) == k]
         for f in FLOWS:
-            for v in range(RING):
-                copy3(q, f, STEPS - 1, v, 1).wait_recv()
-            pair_copy(q, f, STEPS).start()
+            copy3(q, f, step, 1).wait_recv()
+            for at in due:
+                copy3(LINK_ORDER[at][0], f, LINK_ORDER[at][1]).start()
+        for f in FLOWS:
+            pair_copy(q, f, step + 1).start()
 
     def have_pair(q):
         for f in FLOWS:
             for w in range(RING):
                 pair_copy(q, f, w, 1 - core).wait_recv()
 
-    def load(q, i):
-        rows = pl.ds(MATRIX_BASE[q], BLOCK)
-        if q % 2 == 0:
+    def load(up, layer, i):
+        rows = pl.ds(pl.multiple_of(up_base(layer) + (0 if up else BLOCK), CHUNK), BLOCK)
+        if up:
             src = all_ref.at[lax.div(i, 2), :, :, pl.ds(lax.rem(i, 2) * 2, 2), rows]
         else:
             src = all_ref.at[:, i, :, :, rows]
         slot = lax.rem(i, 2)
-        dst = weight.at[slot].reshape(src.shape)
-        return pltpu.make_async_copy(src, dst, load_sem.at[slot])
-
-    def product(q, i):
+        return pltpu.make_async_copy(src, weight.at[slot].reshape(src.shape), load_sem.at[slot])
+
+    def product(up, i):
         slot = lax.rem(i, 2)
         cols = aligned_lanes(i * WIDTH, WIDTH)
-        if q % 2 == 0:
+        if up:
             tiles = weight[slot].reshape(RING * RING, 2, BLOCK, COLS)
             wide = jnp.concatenate([tiles[:, x].reshape(WIDTH, COLS) for x in range(2)], axis=1)
-            hidden = x_ref if q == 0 else hidden_ref
-            act_ref[:, cols] = gelu_fn(jnp.dot(hidden[...], wide, preferred_element_type=F32)).astype(BF16)
+            act_ref[:, cols] = gelu_fn(jnp.dot(hidden_ref[...], wide, preferred_element_type=F32)).astype(BF16)
         else:
             tiles = weight[slot].reshape(2, WIDTH, COLS)
             wide = jnp.concatenate([tiles[c] for c in range(2)], axis=1)
             total[...] += jnp.dot(act_ref[:, cols], wide, preferred_element_type=F32)
 
-    last_step(0)
-    have_pair(0)
-    load(0, 0).start()
-    for q in range(N_MATRICES - 1):
-        if q % 2:
-            total[...] = x_ref[...].astype(F32)
-
-        @pl.loop(0, RING)
-        def _(i):
-            load(q, i).wait()
-
-            @pl.when(i < RING - 1)
+    hidden_ref[...] = x_ref[...]
+    total[...] = x_ref[...].astype(F32)
+
+    @pl.loop(0, len(GROUP_EVENTS))
+    def _(group):
+        matrix, half = lax.div(group, 2), lax.rem(group, 2)
+        layer = lax.div(matrix, 2)
+        for g, (events, ready) in enumerate(GROUP_EVENTS):
+            @pl.when(group == g)
             def _():
-                load(q, i + 1).start()
-
-            @pl.when(i == RING - 1)
+                for k in events:
+                    arrive(k)
+                for q in ready:
+                    have_pair(q)
+
+        for up in (True, False):
+            @pl.when((lax.rem(matrix, 2) == 0) == up)
             def _():
-                have_pair(q + 1)
-                if q + 1 < N_MATRICES - 1:
-                    load(q + 1, 0).start()
-
-            product(q, i)
-
-            @pl.when(i == 1)
-            def _():
-                last_step(q + 1)
-
-        if q % 2:
-            hidden_ref[...] = total[...].astype(BF16)
+                first = half * 2
+                load(up, layer, first).start()
+                load(up, layer, first + 1).start()
+
+                @pl.loop(first, first + 2)
+                def _(i):
+                    load(up, layer, i).wait()
+                    product(up, i)
+
+                if not up:
+                    @pl.when(half == 1)
+                    def _():
+                        hidden_ref[...] = total[...].astype(BF16)
+
+    for k in LAST_EVENTS:
+        arrive(k)
+    have_pair(N_MATRICES - 1)
     for q, f in pieces:
         for step in range(STEPS):
             copy1(q, f, step).wait_send()
             copy2(q, f, step).wait_send()
-            for v in range(RING):
-                copy3(q, f, step, v).wait_send()
+            copy3(q, f, step).wait_send()
         for w in range(RING):
             pair_copy(q, f, w).wait_send()
 
 
 def gather_forward(block, x_next):
     tokens = x_next.shape[0]
-    one, four = SEMS((N_MATRICES, N_FLOWS, STEPS)), SEMS((N_MATRICES, N_FLOWS, STEPS, RING))
+    one = SEMS((N_MATRICES, N_FLOWS, STEPS))
     pair = SEMS((N_MATRICES, N_FLOWS, RING))
     return pl.pallas_call(
         gather_kernel,
@@ -551,7 +560,7 @@
         out_specs=[in_hbm(), in_vmem(), in_vmem()],
         scratch_shapes=[
             pltpu.VMEM((tokens, WIDTH), F32), pltpu.VMEM((2, 2, RING, RING, BLOCK, COLS), BF16),
-            SEMS, SEMS((2,)), one, one, one, one, four, four, pair, pair,
+            SEMS, SEMS((2,)), one, one, one, one, one, one, pair, pair,
         ],
         compiler_params=comm_params(2),
         name="torus_gather_forward",

time: 499 us -> 482 us (0.966); the launches traced: 492 us -> 481 us
  Pallas kernels: 426 us -> 415 us
    pallas_call x1, Pallas kernels: 134 us -> 123 us  [gather_forward(): pl.pallas_call(gather_kernel, out_shape=[jax.ShapeDtypeStruct((2, RING, R...]
where the time goes in v3:
time: 482 us; the launch traced here: 481 us
  Pallas kernels  415 us (86%)
  matrix products  62 us (13%)
    pallas_call x1, Pallas kernels, reduce_blocks(): pl.pallas_call(reduce_kernel, out_shape=[jax.ShapeDtypeStruct((ROWS, COLS...  222 us
    pallas_call x1, Pallas kernels, gather_forward(): pl.pallas_call(gather_kernel, out_shape=[jax.ShapeDtypeStruct((2, RING, R...  123 us
    pallas_call x1, Pallas kernels, update_rows(): pl.pallas_call(update_kernel, out_shape=[jax.ShapeDtypeStruct((ROWS, COLS...  29.6 us
    dot_general x2, matrix products, local_step(): lax.dot_general(grad_cur, w_down[layer_idx], (((1,), (1,)), ((), ())), pr...  28.1 us
    pallas_call x2, Pallas kernels, grad_sum(): pl.pallas_call(grad_kernel, out_shape=jax.ShapeDtypeStruct((zy, RING, 2,...  26.8 us
    dot_general x2, matrix products, local_step(): pre_act = jnp.dot(x_in, w_up[layer_idx], preferred_element_type=F32)  22.5 us
    dot_general x1, matrix products, local_step(): lax.dot_general(d_pre, w_up[layer_idx], (((1,), (1,)), ((), ())), preferr...  11.3 us
    pallas_call x1, Pallas kernels, last_product(): pl.pallas_call(down_kernel, out_shape=jax.ShapeDtypeStruct((tokens, WIDTH...  10.5 us
  transfers between devices with their start and end apart: 4, of which 0 were waited for; matrix products, arithmetic and copies ran while one was open for 8% of the time, Pallas kernels for 3%

profile of v3, /device:TPU:0, one launch (start us, length us, event | category | flops | bytes accessed | tf_op | source)
XLA Modules:
  0.0 481.0 jit_solution(10334019769476167751)
XLA Ops:
  0.6 10.8 %multiply_convert_fusion.1 = (bf16[384,5120]{1,0:T(8,128)(2,1)}, f32[384,5120]{1,0:T(8,128)S(1)}) fusion(bf16[2,1280,5120]{2,1,0:T(8,128)(2,1)} %param.16, bf16[2,1,384,1280]{3,2,1,0:T(8,128)(2,1)} %param.13), kind=kOutput, calls=%fused_computation.34 | convolution fusion | flops 5050859520 | bytes 25886720 | tf_op jit(solution)/shard_map/dot_general | solution.py:855
  11.5 0.0 copy-start.1
  11.5 13.4 %fusion.21.right = bf16[384,5120]{1,0:T(8,128)(2,1)} fusion(f32[384,5120]{1,0:T(8,128)S(1)} %get-tuple-element.44, bf16[2,5120,1280]{2,1,0:T(8,128)(2,1)} %param.17, bf16[1,384,1280]{2,1,0:T(8,128)(2,1)} %param.14), kind=kOutput, calls=%fused_computation.25 | convolution fusion | flops 5072486400 | bytes 25886720 | tf_op jit(solution)/shard_map/dot_general | solution.py:857
  24.9 0.0 collective-permute-start.3
  24.9 0.0 copy-done.1
  24.9 1.1 slice_bitcast_fusion
  26.0 0.0 copy-start
  26.0 0.5 collective-permute-start.2
  26.5 0.0 collective-permute-start
  26.5 0.5 collective-permute-start.1
  27.0 11.7 %multiply_convert_fusion = (bf16[384,5120]{1,0:T(8,128)(2,1)}, f32[384,5120]{1,0:T(8,128)}) fusion(bf16[2,1280,5120]{2,1,0:T(8,128)(2,1)} %param.16, bf16[2,1,384,1280]{3,2,1,0:T(8,128)(2,1)S(1)} %copy-done.1), kind=kOutput, calls=%fused_computation.33 | convolution fusion | flops 5050859520 | bytes 25886720 | tf_op jit(solution)/shard_map/dot_general | solution.py:855
  38.7 0.0 copy-done
  38.7 11.3 %fusion.36.g_own = bf16[384,1280]{1,0:T(8,128)(2,1)S(1)} fusion(bf16[384,5120]{1,0:T(8,128)(2,1)} %fusion.21.right, bf16[2,1280,5120]{2,1,0:T(8,128)(2,1)} %param.16, bf16[1,384,1280]{2,1,0:T(8,128)(2,1)} %param.14), kind=kOutput, calls=%fused_computation.36 | convolution fusion | flops 5034639360 | bytes 19005440 | tf_op jit(solution)/shard_map/dot_general | solution.py:861
  50.1 0.0 copy-start.2
  50.1 14.7 %fusion.28.d_own = bf16[384,5120]{1,0:T(8,128)(2,1)} fusion(f32[384,5120]{1,0:T(8,128)} %get-tuple-element.46, bf16[384,1280]{1,0:T(8,128)(2,1)S(1)} %fusion.36.g_own, bf16[2,5120,1280]{2,1,0:T(8,128)(2,1)} %param.17), kind=kOutput, calls=%fused_computation.32 | convolution fusion | flops 5072486400 | bytes 25886720 | tf_op jit(solution)/shard_map/dot_general | solution.py:857
  64.8 0.0 copy-done.2
  64.8 0.0 collective-permute-done.2.left_pair
  64.8 0.0 copy-start.3
  64.8 1.0 copy-done.3
  65.7 0.0 collective-permute-done.3.right_pair
  65.7 12.6 %grad_up.1.refs_0_ = f32[16,4,2,80,640]{4,3,2,1,0:T(8,128)} custom-call(s32[1]{0:T(128)} %bitcast.core_ref, bf16[384,1280]{1,0:T(8,128)(2,1)} %copy-done, bf16[384,1280]{1,0:T(8,128)(2,1)} %copy-done.3, bf16[384,5120]{1,0:T(8,128)(2,1)} %fusion.21.right, bf16[384,5120]{1,0:T(8,128)(2,1)} %collective-permute-done.3.right_pair), custom_call_target="tpu_custom_call" | custom-call | flops 5033164800 | bytes 17000000 | tf_op jit(solution)/shard_map/grad_up/pallas_call | solution.py:595
  78.3 0.0 collective-permute-done.1.right_pair
  78.3 0.0 collective-permute-done.left_pair
  78.3 14.2 %grad_down.1 = f32[16,4,2,80,640]{4,3,2,1,0:T(8,128)} custom-call(s32[1]{0:T(128)} %bitcast.core_ref, bf16[384,5120]{1,0:T(8,128)(2,1)} %get-tuple-element.43.left, bf16[384,5120]{1,0:T(8,128)(2,1)} %collective-permute-done.left_pair, bf16[384,1280]{1,0:T(8,128)(2,1)} %bitcast.3.right, ...), custom_call_target="tpu_custom_call", output_to_operand_aliasing={{}: (5, {})} | custom-call | flops 5033164800 | bytes 17000000 | tf_op jit(solution)/shard_map/grad_down/pallas_call | solution.py:595
  92.5 222.3 %torus_reduce.1 = (f32[320,640]{1,0:T(8,128)}, f32[4,4,4,160,640]{4,3,2,1,0:T(8,128)}, bf16[384,1280]{1,0:T(8,128)(2,1)}, bf16[384,2560]{1,0:T(8,128)(2,1)}, bf1...) custom-call(f32[4,4,4,160,640]{4,3,2,1,0:T(8,128)} %bitcast.54, bf16[384,1280]{1,0:T(8,128)(2,1)} %get-tuple-element.41.x_own, ...), custom_call_target="tpu_custom_call" | custom-call | tf_op jit(solution)/shard_map/torus_reduce/pallas_call | solution.py:365
  314.8 29.6 %update_rows.1 = (bf16[320,640]{1,0:T(8,128)(2,1)}, f32[10,2,5120]{2,1,0:T(2,128)}, f32[2,40,1280]{2,1,0:T(8,128)}, f32[10,2,5120]{2,1,0:T(2,128)}, f32[2,40,128...) custom-call(f32[320,640]{1,0:T(8,128)} %get-tuple-element.24.block, f32[10,2,5120]{2,1,0:T(2,128)} %bitcast.58, ...), custom_call_target="tpu_custom_call" | custom-call | tf_op jit(solution)/shard_map/update_rows/pallas_call | solution.py:804
  344.5 123.0 %torus_gather_forward.1 = (bf16[2,4,4,4,320,640]{5,4,3,2,1,0:T(8,128)(2,1)}, bf16[384,1280]{1,0:T(8,128)(2,1)}, bf16[384,5120]{1,0:T(8,128)(2,1)}) custom-call(bf16[320,640]{1,0:T(8,128)(2,1)} %get-tuple-element.25.block_ref, bf16[384,1280]{1,0:T(8,128)(2,1)} %bitcast.57), custom_call_target="tpu_custom_call" | custom-call | tf_op jit(solution)/shard_map/torus_gather_forward/pallas_call | solution.py:552
  467.5 10.5 %forward_down.1 = bf16[384,1280]{1,0:T(8,128)(2,1)} custom-call(bf16[384,5120]{1,0:T(8,128)(2,1)} %get-tuple-element.26.act, bf16[2,16,4,4,80,640]{5,4,3,2,1,0:T(8,128)(2,1)} %bitcast.55, bf16[384,1280]{1,0:T(8,128)(2,1)} %get-tuple-element.28.hidden), custom_call_target="tpu_custom_call" | custom-call | tf_op jit(solution)/shard_map/forward_down/pallas_call | solution.py:632
  478.0 3.1 keep.1
Async XLA Ops:
  11.5 13.4 %copy-start.1 = (bf16[2,1,384,1280]{3,2,1,0:T(8,128)(2,1)S(1)}, bf16[2,1,384,1280]{3,2,1,0:T(8,128)(2,1)}, u32[]{:S(2)}) copy-start(bf16[2,1,384,1280]{3,2,1,0:T(8,128)(2,1)} %param.13) | copy-start | bytes 5898244
  24.9 40.8 %collective-permute-start.3 = (bf16[384,5120]{1,0:T(8,128)(2,1)}, bf16[384,5120]{1,0:T(8,128)(2,1)}, u32[]{:S(2)}, u32[]{:S(2)}) collective-permute-start(bf16[384,5120]{1,0:T(8,128)(2,1)} %fusion.21.right), channel_id=1, source_target_pairs={{0,1},{1,0},{2,3},{3,2},{4,5},{5,4},{6,7},{7,6},{8,9},{9,8},{10,11... | collective-permute-start | bytes 11796488 | tf_op jit(solution)/shard_map/ppermute | solution.py:841
  26.0 12.7 %copy-start = (bf16[384,1280]{1,0:T(8,128)(2,1)}, bf16[384,1280]{1,0:T(8,128)(2,1)S(1)}, u32[]{:S(2)}) copy-start(bf16[384,1280]{1,0:T(8,128)(2,1)S(1)} %get-tuple-element.42.left) | copy-start | bytes 2949124
  26.0 38.8 %collective-permute-start.2 = (bf16[384,1280]{1,0:T(8,128)(2,1)S(1)}, bf16[384,1280]{1,0:T(8,128)(2,1)S(1)}, u32[]{:S(2)}, u32[]{:S(2)}) collective-permute-start(bf16[384,1280]{1,0:T(8,128)(2,1)S(1)} %get-tuple-element.42.left), channel_id=1, source_target_pairs={{0,1},{1,0},{2,3},{3,2},{4,5},{5,4},{6,7},{7,6},{8,9},{9,8},{10,11... | collective-permute-start | bytes 2949128 | tf_op jit(solution)/shard_map/ppermute | solution.py:841
  26.5 51.8 %collective-permute-start = (bf16[384,5120]{1,0:T(8,128)(2,1)}, bf16[384,5120]{1,0:T(8,128)(2,1)}, u32[]{:S(2)}, u32[]{:S(2)}) collective-permute-start(bf16[384,5120]{1,0:T(8,128)(2,1)} %get-tuple-element.43.left), channel_id=1, source_target_pairs={{0,1},{1,0},{2,3},{3,2},{4,5},{5,4},{6,7},{7,6},{8,9},{9,8},{10,11... | collective-permute-start | bytes 11796488 | tf_op jit(solution)/shard_map/ppermute | solution.py:841
  26.5 51.8 %collective-permute-start.1 = (bf16[384,1280]{1,0:T(8,128)(2,1)}, bf16[384,1280]{1,0:T(8,128)(2,1)}, u32[]{:S(2)}, u32[]{:S(2)}) collective-permute-start(bf16[384,1280]{1,0:T(8,128)(2,1)} %bitcast.3.right), channel_id=1, source_target_pairs={{0,1},{1,0},{2,3},{3,2},{4,5},{5,4},{6,7},{7,6},{8,9},{9,8},{10,11... | collective-permute-start | bytes 2949128 | tf_op jit(solution)/shard_map/ppermute | solution.py:841
  50.1 14.7 %copy-start.2 = (bf16[384,1280]{1,0:T(8,128)(2,1)}, bf16[384,1280]{1,0:T(8,128)(2,1)S(1)}, u32[]{:S(2)}) copy-start(bf16[384,1280]{1,0:T(8,128)(2,1)S(1)} %fusion.36.g_own) | copy-start | bytes 2949124
  64.8 1.0 copy-start.3

commit v4 on v3

--- a/solution.py
+++ b/solution.py
@@ -43,9 +43,11 @@
 STEPS = RING - 1
 BATCH_LEN = [[TICKS if f // 2 == b else TICKS - 1 for f in FLOWS] for b in range(LAYERS)]
 BATCH_START = [[sum(lens[:f]) for f in FLOWS] for lens in BATCH_LEN]
-OWN_SLOTS = 3
+OWN_SLOTS = 2
 UP_TILES = 8
 TILES = 16
+GELU_TICK, SUM_TICK = 2, 6
+CARRY_JOBS, GELU_JOBS, SUM_JOBS = 4, 2, 3
 
 
 def up_base(layer):
@@ -126,8 +128,9 @@
 
 
 def reduce_kernel(
-    s_last, x_own, d_own, a_own, g_own, out_ref, s_first, x_pair, d_pair, a_pair, g_pair,
-    recv1, recv2, recv3, own, left, left_pair, right, right_pair, tile, own_sem, tile_in, tile_out, pair_send, pair_got, credit,
+    s_last, x_own, g_last, d_last, w_up, w_down, out_ref, s_first, x_pair, d_own, d_pair, a_own, a_pair, g_pair,
+    recv1, recv2, recv3, own, left, left_pair, right, right_pair, tile, w_tile, w_tile_down, g_own,
+    own_sem, tile_in, tile_out, side_send, side_got, act_send, act_got, d_send, d_got, act_out, d_out, credit,
     send1, got1, send2, got2, send3, got3,
 ):
     core, pos = my_place()
@@ -151,7 +154,7 @@
         return ref.at[j] if second < third else ref.at[:, j]
 
     def slot1(b, step):
-        return step + b * 2 * ((step + 1) // 2)
+        return step + b * (step // 2)
 
     def land1(b, step, chunk):
         return recv1.at[slot1(b, step), chunk]
@@ -239,12 +242,98 @@
         each(add)
         each(pass_on)
 
+    tokens = x_own.shape[0]
+    other = 1 - core
+
+    def back_reads(job, early):
+        slot = lax.rem(job, 2)
+        if early:
+            cols = aligned_lanes(job * COLS, COLS)
+            reads = ((w_up.at[LAYERS - 1, :, cols], w_tile), (d_last.at[:, cols], left))
+        else:
+            cols = aligned_lanes((job - UP_TILES) * COLS, COLS)
+            reads = ((w_up.at[0, :, cols], w_tile), (w_down.at[0, cols], w_tile_down))
+        return [pltpu.make_async_copy(src, dst.at[slot], tile_in.at[i, slot]) for i, (src, dst) in enumerate(reads)]
+
+    def start_back_reads(job):
+        for early in (True, False):
+            @pl.when((job < UP_TILES) if early else (job >= UP_TILES) & (job < TILES))
+            def _():
+                for read in back_reads(job, early):
+                    read.start()
+
+    def transposed(lhs, rhs):
+        return lax.dot_general(lhs, rhs, (((1,), (1,)), ((), ())), preferred_element_type=F32)
+
+    def carry_gradient(job):
+        slot = lax.rem(job, 2)
+        start_back_reads(job + 1)
+        for read in back_reads(slot, True):
+            read.wait()
+        for half in range(2):
+            at = pl.ds(half * COLS, COLS)
+            tile[half, pl.ds(0, tokens)] += transposed(left[slot], w_tile[slot, at])
+
+    def act_copies(i):
+        slot, cols = lax.rem(i, 2), aligned_lanes(i * COLS, COLS)
+        src = right.at[slot]
+        return pltpu.make_async_copy(src, a_own.at[:, cols], act_out.at[slot]), remote(src, a_pair.at[:, cols], act_send.at[slot], act_got.at[i], partner)
+
+    def d_local(i):
+        slot = lax.rem(i, 2)
+        return pltpu.make_async_copy(right_pair.at[slot], d_own.at[:, aligned_lanes(lax.rem(i, RING) * COLS, COLS)], d_out.at[slot])
+
+    def d_remote(i):
+        slot, at = lax.rem(i, 2), lax.rem(i, RING)
+        return remote(right_pair.at[slot], d_pair.at[:, aligned_lanes(at * COLS, COLS)], d_send.at[slot], d_got.at[at], partner)
+
+    def wait_back_writes(i):
+        own_act, pair_act = act_copies(i)
+        own_act.wait()
+        pair_act.wait_send()
+        mine = lax.div(i, RING) == core
+
+        @pl.when(mine)
+        def _():
+            d_local(i).wait()
+
+        @pl.when(jnp.logical_not(mine))
+        def _():
+            d_remote(i).wait_send()
+
+    def through_gelu(i):
+        slot = lax.rem(i, 2)
+        start_back_reads(i + UP_TILES + 1)
+        for read in back_reads(UP_TILES + slot, False):
+            read.wait()
+        pre_act = jnp.dot(x_own[...], w_tile[slot], preferred_element_type=F32)
+        act, gelu_vjp = jax.vjp(gelu_fn, pre_act)
+        d_pre = gelu_vjp(transposed(g_own[...], w_tile_down[slot]))[0]
+
+        @pl.when(i >= 2)
+        def _():
+            wait_back_writes(i - 2)
+
+        right[slot] = act.astype(BF16)
+        right_pair[slot] = d_pre.astype(BF16)
+        for write in act_copies(i):
+            write.start()
+        mine = lax.div(i, RING) == core
+
+        @pl.when(mine)
+        def _():
+            d_local(i).start()
+
+        @pl.when(jnp.logical_not(mine))
+        def _():
+            d_remote(i).start()
+
     def tile_reads(job, up):
         slot = lax.rem(job, 2)
         if up:
             rows = aligned_lanes(lax.div(job, RING) * COLS, COLS)
-            cols = lax.rem(job, RING) * COLS
-            reads = (x_own.at[:, rows], x_pair.at[:, rows], d_own.at[:, aligned_lanes(core * (FF // 2) + cols, COLS)], d_pair.at[:, aligned_lanes(cols, COLS)])
+            cols = aligned_lanes(lax.rem(job, RING) * COLS, COLS)
+            reads = (x_own.at[:, rows], x_pair.at[:, rows], d_own.at[:, cols], d_pair.at[:, cols])
         else:
             rows = aligned_lanes((job - UP_TILES) * COLS, COLS)
             reads = (a_own.at[:, rows], a_pair.at[:, rows], g_own.at[:, aligned_lanes(core * COLS, COLS)], g_pair)
@@ -267,7 +356,7 @@
         else:
             i = job - UP_TILES
             dst = s_first.at[lax.div(i, 2), pl.ds(lax.rem(i, 2) * 2, 2), :, pl.ds(BLOCK, BLOCK)]
-        return pltpu.make_async_copy(tile.at[slot], dst, tile_out.at[slot])
+        return pltpu.make_async_copy(tile.at[slot].reshape(dst.shape), dst, tile_out.at[slot])
 
     def compute(job):
         slot = lax.rem(job, 2)
@@ -279,54 +368,75 @@
         def _():
             tile_write(UP_TILES + slot, False).wait()
 
-        total = rounded_product(left[slot], right[slot]) + rounded_product(left_pair[slot], right_pair[slot])
-        tile[slot] = total.reshape(tile.shape[1:])
+        tile[slot] = rounded_product(left[slot], right[slot]) + rounded_product(left_pair[slot], right_pair[slot])
         for up in (True, False):
             @pl.when((job < UP_TILES) if up else (job >= UP_TILES))
             def _():
                 tile_write(job, up).start()
 
+    def side_copy(i):
+        src, dst = ((x_own, x_pair), (g_own.at[:, aligned_lanes(other * COLS, COLS)], g_pair))[i]
+        return remote(src, dst, side_send.at[i], side_got.at[i], partner)
+
     start_batch(0)
-    other = 1 - core
-    gives = (x_own, d_own.at[:, aligned_lanes(other * (FF // 2), FF // 2)], a_own, g_own.at[:, aligned_lanes(other * COLS, COLS)])
-    exchange = [
-        remote(src, dst, pair_send.at[i], pair_got.at[i], partner)
-        for i, (src, dst) in enumerate(zip(gives, (x_pair, d_pair, a_pair, g_pair)))
-    ]
-    for give in exchange:
-        give.start()
-    for give in exchange:
-        give.wait_recv()
-    start_reads(0)
-
-    @pl.loop(0, 2 * TICKS)
+    side_copy(0).start()
+    start_back_reads(0)
+    for half in range(2):
+        tile[half, pl.ds(0, tokens)] = g_last[:, pl.ds(half * COLS, COLS)].astype(F32)
+
+    @pl.loop(0, STEPS * TICKS)
     def _(n):
         tick(0, 0, n)
 
-        @pl.loop(0, 2)
-        def _(i):
-            compute(2 * n + i)
+        @pl.when(n < GELU_TICK)
+        def _():
+            @pl.loop(0, CARRY_JOBS)
+            def _(i):
+                carry_gradient(n * CARRY_JOBS + i)
+
+        @pl.when(n == GELU_TICK - 1)
+        def _():
+            for half in range(2):
+                g_own[:, pl.ds(half * COLS, COLS)] = tile[half, pl.ds(0, tokens)].astype(BF16)
+
+        @pl.when((n >= GELU_TICK) & (n < SUM_TICK))
+        def _():
+            @pl.loop(0, GELU_JOBS)
+            def _(i):
+                through_gelu((n - GELU_TICK) * GELU_JOBS + i)
+
+        @pl.when(n == GELU_TICK)
+        def _():
+            side_copy(1).start()
+
+        @pl.when(n == SUM_TICK)
+        def _():
+            for i in range(2):
+                wait_back_writes(UP_TILES - 2 + i)
+                side_copy(i).wait_recv()
+            for i in range(UP_TILES):
+                act_copies(i)[1].wait_recv()
+            for i in range(RING):
+                d_remote(i).wait_recv()
+            start_reads(0)
+
+        @pl.when(n >= SUM_TICK)
+        def _():
+            @pl.loop(0, SUM_JOBS)
+            def _(i):
+                job = (n - SUM_TICK) * SUM_JOBS + i
+                pl.when(job < TILES)(functools.partial(compute, job))
 
     for slot in range(2):
         tile_write(UP_TILES + slot, False).wait()
     for f in FLOWS:
         for k in range(BATCH_LEN[0][f]):
-            copy(0, 0, f, 1, BATCH_START[0][f] + k, None).wait_send()
+            for step in range(1, STEPS):
+                copy(0, 0, f, step, BATCH_START[0][f] + k, None).wait_send()
         pl.semaphore_signal(credit.at[f], inc=1, device_id=(source[f],), device_id_type=MESH)
     for f in FLOWS:
         pl.semaphore_wait(credit.at[f], 1)
-    for k in range(TICKS):
-        for f in FLOWS:
-            if k < BATCH_LEN[1][f]:
-                first_copy(0, 1, f, BATCH_START[1][f] + k).start()
-
-    @pl.loop(2 * TICKS, STEPS * TICKS)
-    def _(n):
-        tick(0, 0, n)
-
-    for n in range(OWN_SLOTS - 1):
-        for f in FLOWS:
-            own_copy(1, f, n).start()
+    start_batch(1)
 
     @pl.loop(0, STEPS * TICKS)
     def _(n):
@@ -342,19 +452,19 @@
     def _(n):
         tick(2, 1, n)
 
-    for give in exchange:
-        give.wait_send()
+    for i in range(2):
+        side_copy(i).wait_send()
     for b in range(LAYERS):
         for f in FLOWS:
             @pl.loop(BATCH_START[b][f], BATCH_START[b][f] + BATCH_LEN[b][f])
             def _(chunk):
                 for phase in range(3):
                     for step in range(STEPS):
-                        if (phase, b, step) != (0, 0, 1):
+                        if step == 0 or phase + b:
                             copy(phase, b, f, step, chunk, None).wait_send()
 
 
-def reduce_blocks(s_last, x_first, d_first, a_first, g_first):
+def reduce_blocks(s_last, x_first, g_last, d_last, w_up, w_down):
     tokens = x_first.shape[0]
 
     def half(width):
@@ -362,24 +472,28 @@
 
     piece = pltpu.VMEM((2, tokens, COLS), BF16)
     sems = SEMS((LAYERS, STEPS, BATCH_CHUNKS))
+    two, tiles = SEMS((2,)), SEMS((UP_TILES,))
+    spaces = [half(WIDTH), half(FF // 2), half(FF // 2), half(FF), half(FF), half(COLS)]
     return pl.pallas_call(
         reduce_kernel,
-        out_shape=[jax.ShapeDtypeStruct((ROWS, COLS), F32), jax.ShapeDtypeStruct(s_last.shape, F32), half(WIDTH), half(FF // 2), half(FF), half(COLS)],
-        in_specs=[in_hbm()] * 5,
-        out_specs=[in_vmem()] + [in_hbm()] * 5,
+        out_shape=[jax.ShapeDtypeStruct((ROWS, COLS), F32), jax.ShapeDtypeStruct(s_last.shape, F32)] + spaces,
+        in_specs=[in_hbm(), in_vmem(), in_vmem(), in_hbm(), in_hbm(), in_hbm()],
+        out_specs=[in_vmem(), in_hbm()] + [in_hbm()] * len(spaces),
         scratch_shapes=[
-            pltpu.VMEM((5, BATCH_CHUNKS, RING, RING, CHUNK, COLS), F32),
+            pltpu.VMEM((RING, BATCH_CHUNKS, RING, RING, CHUNK, COLS), F32),
             pltpu.VMEM((LAYERS, STEPS, BATCH_CHUNKS, RING, CHUNK, COLS), F32),
             pltpu.VMEM((LAYERS, STEPS, BATCH_CHUNKS, CHUNK, COLS), F32),
             pltpu.VMEM((N_FLOWS, OWN_SLOTS, RING, RING, CHUNK, COLS), F32),
             piece, piece, piece, piece,
-            pltpu.VMEM((2, 2, RING, BLOCK, COLS), F32),
-            SEMS((N_FLOWS, OWN_SLOTS)), SEMS((4, 2)), SEMS((2,)), SEMS((4,)), SEMS((4,)), pltpu.SemaphoreType.REGULAR((N_FLOWS,)),
+            pltpu.VMEM((2, COLS, COLS), F32), pltpu.VMEM((2, WIDTH, COLS), BF16), pltpu.VMEM((2, COLS, WIDTH), BF16),
+            pltpu.VMEM((tokens, WIDTH), BF16),
+            SEMS((N_FLOWS, OWN_SLOTS)), SEMS((RING, 2)), two, two, two, two, tiles, two, SEMS((RING,)), two, two,
+            pltpu.SemaphoreType.REGULAR((N_FLOWS,)),
             sems, sems, sems, sems, sems, sems,
         ],
         compiler_params=comm_params(1),
         name="torus_reduce",
-    )(s_last, x_first, d_first, a_first, g_first)[0]
+    )(s_last, x_first, g_last, d_last, w_up, w_down)[0]
 
 
 N_MATRICES = 2 * LAYERS
@@ -578,10 +692,10 @@
             out[:, x, 0] = total[:, COLS * x:COLS * (x + 1)].reshape(-1, BLOCK, COLS)
 
 
-def grad_sum(core, left, left_pair, right, right_pair, sums):
+def grad_sum(core, left, left_pair, right, right_pair, sums, up):
     tokens = left.shape[0]
     zy = RING * RING
-    if sums is None:
+    if up:
         grid = (2, 2)
         left_spec = pl.BlockSpec((tokens, COLS), lambda i, x, c: (0, i))
         right_spec = pl.BlockSpec((tokens, 2 * COLS), lambda i, x, c: (0, c[0] * 2 + x))
@@ -604,7 +718,7 @@
         input_output_aliases={5: 0} if before else {},
         compiler_params=plain_params(len(grid)),
         cost_estimate=pl.CostEstimate(flops=2 * tokens * WIDTH * FF, bytes_accessed=17_000_000, transcendentals=0),
-        name="grad_up" if sums is None else "grad_down",
+        name="grad_up" if up else "grad_down",
     )(core, left, left_pair, right, right_pair, *before)
 
 
@@ -848,21 +962,16 @@
 def local_step(x_saved, grad_out, x_next, w_up, w_down, gacc_up, gacc_down, master_up, master_down, mom1_up, mom1_down, mom2_up, mom2_down):
     core = jnp.reshape(lax.rem(lax.axis_index("fsdp"), 2), (1,))
     x_tokens = x_saved.reshape(LAYERS, -1, WIDTH)
-    grad_cur = grad_out.reshape(-1, WIDTH)
-    operands = []
-    for layer_idx in range(LAYERS - 1, -1, -1):
-        x_in = x_tokens[layer_idx]
-        pre_act = jnp.dot(x_in, w_up[layer_idx], preferred_element_type=F32)
-        hidden_act, gelu_vjp = jax.vjp(gelu_fn, pre_act)
-        d_act = lax.dot_general(grad_cur, w_down[layer_idx], (((1,), (1,)), ((), ())), preferred_element_type=F32)
-        d_pre = gelu_vjp(d_act)[0].astype(BF16)
-        operands.append((x_in, d_pre, hidden_act.astype(BF16), grad_cur))
-        if layer_idx > 0:
-            grad_cur = (grad_cur.astype(F32) + lax.dot_general(d_pre, w_up[layer_idx], (((1,), (1,)), ((), ())), preferred_element_type=F32)).astype(BF16)
-    x_last, d_last, a_last, g_last = operands[0]
-    sums = grad_sum(core, x_last, swap_cores(x_last), d_last, swap_cores(d_last), None)
-    sums = grad_sum(core, a_last, swap_cores(a_last), g_last, swap_cores(g_last), sums)
-    block = reduce_blocks(sums.reshape(RING, RING, RING, PAIR_ROWS, COLS), *operands[1])
+    grad_last = grad_out.reshape(-1, WIDTH)
+    x_last = x_tokens[LAYERS - 1]
+    pre_act = jnp.dot(x_last, w_up[LAYERS - 1], preferred_element_type=F32)
+    hidden_act, gelu_vjp = jax.vjp(gelu_fn, pre_act)
+    act_last = hidden_act.astype(BF16)
+    d_act = lax.dot_general(grad_last, w_down[LAYERS - 1], (((1,), (1,)), ((), ())), preferred_element_type=F32)
+    d_last = gelu_vjp(d_act)[0].astype(BF16)
+    sums = grad_sum(core, act_last, swap_cores(act_last), grad_last, swap_cores(grad_last), None, False)
+    sums = grad_sum(core, x_last, swap_cores(x_last), d_last, swap_cores(d_last), sums, True)
+    block = reduce_blocks(sums.reshape(RING, RING, RING, PAIR_ROWS, COLS), x_tokens[0], grad_last, d_last, w_up, w_down)
 
     new_block, *state = update_rows(
         block, rows_first(gacc_up), gacc_down, rows_first(master_up), master_down,

time: 482 us -> 471 us (0.977)
  matrix products: 62 us -> 26.3 us
  Pallas kernels: 415 us -> 434 us
  waiting for transfers between devices: 0.01 us -> 5.91 us
    dot_general x5 -> x2, matrix products: 62 us -> 26.3 us  [the longest x1 14.3 us: local_step(): lax.dot_general(grad_last, w_down[LAYERS - 1], (((1,), (1,)), ((), ())),...]
    pallas_call x1, Pallas kernels: 222 us -> 240 us  [reduce_blocks(): pl.pallas_call(reduce_kernel, out_shape=[jax.ShapeDtypeStruct((ROWS, COLS...]
    ppermute x4, waiting for transfers between devices: 0.01 us -> 5.91 us  [swap_cores(): return lax.ppermute(array, 'fsdp', SWAP)]
  transfers between devices with their start and end apart: 4 -> 4, of which waited for: 0 -> 1; matrix products, arithmetic and copies ran while one was open for 8% -> 3% of each run, Pallas kernels for 3% -> 3%
where the time goes in v4:
time: 471 us; the launch traced here: 470 us
  Pallas kernels  434 us (92%)
  matrix products  26.3 us (6%)
  waiting for transfers between devices  5.91 us (1%)
    pallas_call x1, Pallas kernels, reduce_blocks(): pl.pallas_call(reduce_kernel, out_shape=[jax.ShapeDtypeStruct((ROWS, COLS...  240 us
    pallas_call x1, Pallas kernels, gather_forward(): pl.pallas_call(gather_kernel, out_shape=[jax.ShapeDtypeStruct((2, RING, R...  123 us
    pallas_call x1, Pallas kernels, update_rows(): pl.pallas_call(update_kernel, out_shape=[jax.ShapeDtypeStruct((ROWS, COLS...  30.8 us
    pallas_call x2, Pallas kernels, grad_sum(): pl.pallas_call(grad_kernel, out_shape=jax.ShapeDtypeStruct((zy, RING, 2,...  26.6 us
    dot_general x1, matrix products, local_step(): lax.dot_general(grad_last, w_down[LAYERS - 1], (((1,), (1,)), ((), ())),...  14.3 us
    dot_general x1, matrix products, local_step(): pre_act = jnp.dot(x_last, w_up[LAYERS - 1], preferred_element_type=F32)  12 us
    pallas_call x1, Pallas kernels, last_product(): pl.pallas_call(down_kernel, out_shape=jax.ShapeDtypeStruct((tokens, WIDTH...  10.5 us
  transfers between devices with their start and end apart: 4, of which 1 were waited for; matrix products, arithmetic and copies ran while one was open for 3% of the time, Pallas kernels for 3%

profile of v4, /device:TPU:0, one launch (start us, length us, event | category | flops | bytes accessed | tf_op | source)
XLA Modules:
  0.0 470.3 jit_solution(6244658740157473321)
XLA Ops:
  0.6 0.0 copy-start
  0.6 12.0 %multiply_convert_fusion = (bf16[384,5120]{1,0:T(8,128)(2,1)}, f32[384,5120]{1,0:T(8,128)}) fusion(bf16[2,1280,5120]{2,1,0:T(8,128)(2,1)} %w_up.1, bf16[2,1,384,1280]{3,2,1,0:T(8,128)(2,1)} %param.13), kind=kOutput, calls=%fused_computation.15 | convolution fusion | flops 5050859520 | bytes 25886720 | tf_op jit(solution)/shard_map/dot_general | solution.py:967
  12.6 0.0 collective-permute-start.2
  12.6 0.0 copy-done
  12.6 0.0 copy-start.1
  12.6 14.3 %fusion.12.right.d_last = bf16[384,5120]{1,0:T(8,128)(2,1)} fusion(f32[384,5120]{1,0:T(8,128)} %get-tuple-element.44, bf16[2,5120,1280]{2,1,0:T(8,128)(2,1)} %w_down.1, bf16[1,384,1280]{2,1,0:T(8,128)(2,1)S(1)} %copy-done), kind=kOutput, calls=%fused_computation.14 | convolution fusion | flops 5072486400 | bytes 25886720 | tf_op jit(solution)/shard_map/dot_general | solution.py:970
  26.9 0.5 collective-permute-start.1
  27.4 0.0 collective-permute-start.3
  27.5 0.0 copy-done.1
  27.5 1.4 slice_bitcast_fusion
  28.9 0.5 collective-permute-start
  29.3 5.9 %collective-permute-done.3.right_pair = bf16[384,1280]{1,0:T(8,128)(2,1)S(1)} collective-permute-done((bf16[384,1280]{1,0:T(8,128)(2,1)S(1)}, bf16[384,1280]{1,0:T(8,128)(2,1)S(1)}, u32[]{:S(2)}, u32[]{:S(2)}) %collective-permute-start.3) | collective-permute-done | bytes 983072 | tf_op jit(solution)/shard_map/ppermute | solution.py:955
  35.3 0.0 copy-start.2
  35.3 0.9 copy-done.2
  36.2 0.0 collective-permute-done.2.left_pair
  36.2 13.9 %grad_down.1.refs_0_ = f32[16,4,2,80,640]{4,3,2,1,0:T(8,128)} custom-call(s32[1]{0:T(128)} %bitcast.core_ref, bf16[384,5120]{1,0:T(8,128)(2,1)} %get-tuple-element.43.left, bf16[384,5120]{1,0:T(8,128)(2,1)} %collective-permute-done.2.left_pair, bf16[384,1280]{1,0:T(8,128)(2,1)} %bitcast.34, bf16[384,1280]{1,0:T(8,128)(2,1)} %copy-done.2), custom_call_target="tpu_custom_call" | custom-call | flops 5033164800 | bytes 17000000 | tf_op jit(solution)/shard_map/grad_down/pallas_call | solution.py:709
  50.1 0.0 collective-permute-done.left_pair
  50.1 0.0 collective-permute-done.1.right_pair
  50.2 12.6 %grad_up.1 = f32[16,4,2,80,640]{4,3,2,1,0:T(8,128)} custom-call(s32[1]{0:T(128)} %bitcast.core_ref, bf16[384,1280]{1,0:T(8,128)(2,1)} %get-tuple-element.42.left, bf16[384,1280]{1,0:T(8,128)(2,1)} %collective-permute-done.left_pair, bf16[384,5120]{1,0:T(8,128)(2,1)} %fusion.12.right.d_last, ...), custom_call_target="tpu_custom_call", output_to_operand_aliasing={{}: (5, {})} | custom-call | flops 5033164800 | bytes 17000000 | tf_op jit(solution)/shard_map/grad_up/pallas_call | solution.py:709
  62.8 239.9 %torus_reduce.1 = (f32[320,640]{1,0:T(8,128)}, f32[4,4,4,160,640]{4,3,2,1,0:T(8,128)}, bf16[384,1280]{1,0:T(8,128)(2,1)}, bf16[384,2560]{1,0:T(8,128)(2,1)}, bf1...) custom-call(f32[4,4,4,160,640]{4,3,2,1,0:T(8,128)} %bitcast.32, ...), custom_call_target="tpu_custom_call" | custom-call | tf_op jit(solution)/shard_map/torus_reduce/pallas_call | solution.py:477
  302.7 30.8 %update_rows.1 = (bf16[320,640]{1,0:T(8,128)(2,1)}, f32[10,2,5120]{2,1,0:T(2,128)}, f32[2,40,1280]{2,1,0:T(8,128)}, f32[10,2,5120]{2,1,0:T(2,128)}, f32[2,40,128...) custom-call(f32[320,640]{1,0:T(8,128)} %get-tuple-element.24.block, f32[10,2,5120]{2,1,0:T(2,128)} %bitcast.39, ...), custom_call_target="tpu_custom_call" | custom-call | tf_op jit(solution)/shard_map/update_rows/pallas_call | solution.py:918
  333.5 123.3 %torus_gather_forward.1 = (bf16[2,4,4,4,320,640]{5,4,3,2,1,0:T(8,128)(2,1)}, bf16[384,1280]{1,0:T(8,128)(2,1)}, bf16[384,5120]{1,0:T(8,128)(2,1)}) custom-call(bf16[320,640]{1,0:T(8,128)(2,1)} %get-tuple-element.25.block_ref, bf16[384,1280]{1,0:T(8,128)(2,1)} %bitcast.38), custom_call_target="tpu_custom_call" | custom-call | tf_op jit(solution)/shard_map/torus_gather_forward/pallas_call | solution.py:666
  456.8 10.5 %forward_down.1 = bf16[384,1280]{1,0:T(8,128)(2,1)} custom-call(bf16[384,5120]{1,0:T(8,128)(2,1)} %get-tuple-element.26.act, bf16[2,16,4,4,80,640]{5,4,3,2,1,0:T(8,128)(2,1)} %bitcast.33, bf16[384,1280]{1,0:T(8,128)(2,1)} %get-tuple-element.28.hidden), custom_call_target="tpu_custom_call" | custom-call | tf_op jit(solution)/shard_map/forward_down/pallas_call | solution.py:746
  467.2 3.1 keep.1
Async XLA Ops:
  0.6 12.0 %copy-start = (bf16[1,384,1280]{2,1,0:T(8,128)(2,1)S(1)}, bf16[1,384,1280]{2,1,0:T(8,128)(2,1)}, u32[]{:S(2)}) copy-start(bf16[1,384,1280]{2,1,0:T(8,128)(2,1)} %param.14) | copy-start | bytes 2949124
  12.6 23.6 %collective-permute-start.2 = (bf16[384,5120]{1,0:T(8,128)(2,1)}, bf16[384,5120]{1,0:T(8,128)(2,1)}, u32[]{:S(2)}, u32[]{:S(2)}) collective-permute-start(bf16[384,5120]{1,0:T(8,128)(2,1)} %get-tuple-element.43.left), channel_id=1, source_target_pairs={{0,1},{1,0},{2,3},{3,2},{4,5},{5,4},{6,7},{7,6},{8,9},{9,8},{10,11... | collective-permute-start | bytes 11796488 | tf_op jit(solution)/shard_map/ppermute | solution.py:955
  12.6 14.9 %copy-start.1 = (bf16[2,1,384,1280]{3,2,1,0:T(8,128)(2,1)S(1)}, bf16[2,1,384,1280]{3,2,1,0:T(8,128)(2,1)}, u32[]{:S(2)}) copy-start(bf16[2,1,384,1280]{3,2,1,0:T(8,128)(2,1)} %param.13) | copy-start | bytes 5898244
  26.9 23.2 %collective-permute-start.1 = (bf16[384,5120]{1,0:T(8,128)(2,1)}, bf16[384,5120]{1,0:T(8,128)(2,1)}, u32[]{:S(2)}, u32[]{:S(2)}) collective-permute-start(bf16[384,5120]{1,0:T(8,128)(2,1)} %fusion.12.right.d_last), channel_id=1, source_target_pairs={{0,1},{1,0},{2,3},{3,2},{4,5},{5,4},{6,7},{7,6},{8,9},{9,8},{10,11... | collective-permute-start | bytes 11796488 | tf_op jit(solution)/shard_map/ppermute | solution.py:955
  27.4 7.8 %collective-permute-start.3 = (bf16[384,1280]{1,0:T(8,128)(2,1)S(1)}, bf16[384,1280]{1,0:T(8,128)(2,1)S(1)}, u32[]{:S(2)}, u32[]{:S(2)}) collective-permute-start(bf16[384,1280]{1,0:T(8,128)(2,1)S(1)} %bitcast.36), channel_id=1, source_target_pairs={{0,1},{1,0},{2,3},{3,2},{4,5},{5,4},{6,7},{7,6},{8,9},{9,8},{10,11... | collective-permute-start | bytes 2949128 | tf_op jit(solution)/shard_map/ppermute | solution.py:955
  28.9 21.3 %collective-permute-start = (bf16[384,1280]{1,0:T(8,128)(2,1)}, bf16[384,1280]{1,0:T(8,128)(2,1)}, u32[]{:S(2)}, u32[]{:S(2)}) collective-permute-start(bf16[384,1280]{1,0:T(8,128)(2,1)} %get-tuple-element.42.left), channel_id=1, source_target_pairs={{0,1},{1,0},{2,3},{3,2},{4,5},{5,4},{6,7},{7,6},{8,9},{9,8},{10,11... | collective-permute-start | bytes 2949128 | tf_op jit(solution)/shard_map/ppermute | solution.py:955
  35.3 0.9 copy-start.2

commit v5 on v4

--- a/solution.py
+++ b/solution.py
@@ -47,7 +47,7 @@
 UP_TILES = 8
 TILES = 16
 GELU_TICK, SUM_TICK = 2, 6
-CARRY_JOBS, GELU_JOBS, SUM_JOBS = 4, 2, 3
+CARRY_JOBS, GELU_JOBS = 4, 2
 
 
 def up_base(layer):
@@ -422,18 +422,22 @@
 
         @pl.when(n >= SUM_TICK)
         def _():
-            @pl.loop(0, SUM_JOBS)
-            def _(i):
-                job = (n - SUM_TICK) * SUM_JOBS + i
-                pl.when(job < TILES)(functools.partial(compute, job))
-
-    for slot in range(2):
-        tile_write(UP_TILES + slot, False).wait()
+            compute(n - SUM_TICK)
+
     for f in FLOWS:
         for k in range(BATCH_LEN[0][f]):
             for step in range(1, STEPS):
                 copy(0, 0, f, step, BATCH_START[0][f] + k, None).wait_send()
         pl.semaphore_signal(credit.at[f], inc=1, device_id=(source[f],), device_id_type=MESH)
+
+    @pl.loop(0, STEPS * TICKS)
+    def _(n):
+        tick(1, 0, n)
+        job = n + STEPS * TICKS - SUM_TICK
+        pl.when(job < TILES)(functools.partial(compute, job))
+
+    for slot in range(2):
+        tile_write(UP_TILES + slot, False).wait()
     for f in FLOWS:
         pl.semaphore_wait(credit.at[f], 1)
     start_batch(1)
@@ -441,12 +445,11 @@
     @pl.loop(0, STEPS * TICKS)
     def _(n):
         tick(0, 1, n)
-        tick(1, 0, n)
+        tick(2, 0, n)
 
     @pl.loop(0, STEPS * TICKS)
     def _(n):
         tick(1, 1, n)
-        tick(2, 0, n)
 
     @pl.loop(0, STEPS * TICKS)
     def _(n):
@@ -969,8 +972,9 @@
     act_last = hidden_act.astype(BF16)
     d_act = lax.dot_general(grad_last, w_down[LAYERS - 1], (((1,), (1,)), ((), ())), preferred_element_type=F32)
     d_last = gelu_vjp(d_act)[0].astype(BF16)
-    sums = grad_sum(core, act_last, swap_cores(act_last), grad_last, swap_cores(grad_last), None, False)
-    sums = grad_sum(core, x_last, swap_cores(x_last), d_last, swap_cores(d_last), sums, True)
+    d_sent, x_pair, g_pair = lax.optimization_barrier((d_last, swap_cores(x_last), swap_cores(grad_last)))
+    sums = grad_sum(core, act_last, swap_cores(act_last), grad_last, g_pair, None, False)
+    sums = grad_sum(core, x_last, x_pair, d_last, swap_cores(d_sent), sums, True)
     block = reduce_blocks(sums.reshape(RING, RING, RING, PAIR_ROWS, COLS), x_tokens[0], grad_last, d_last, w_up, w_down)
 
     new_block, *state = update_rows(

time: 471 us -> 464 us (0.985)
  waiting for transfers between devices: 5.91 us -> 0.01 us
    ppermute x4, waiting for transfers between devices: 5.91 us -> 0.01 us  [swap_cores(): return lax.ppermute(array, 'fsdp', SWAP)]
  transfers between devices with their start and end apart: 4 -> 4, of which waited for: 1 -> 0; matrix products, arithmetic and copies ran while one was open for 3% -> 6% of each run, Pallas kernels for 3% -> 3%
where the time goes in v5:
time: 464 us; the launch traced here: 463 us
  Pallas kernels  434 us (94%)
  matrix products  23.9 us (5%)
    pallas_call x1, Pallas kernels, reduce_blocks(): pl.pallas_call(reduce_kernel, out_shape=[jax.ShapeDtypeStruct((ROWS, COLS...  241 us
    pallas_call x1, Pallas kernels, gather_forward(): pl.pallas_call(gather_kernel, out_shape=[jax.ShapeDtypeStruct((2, RING, R...  123 us
    pallas_call x1, Pallas kernels, update_rows(): pl.pallas_call(update_kernel, out_shape=[jax.ShapeDtypeStruct((ROWS, COLS...  29.6 us
    pallas_call x2, Pallas kernels, grad_sum(): pl.pallas_call(grad_kernel, out_shape=jax.ShapeDtypeStruct((zy, RING, 2,...  26.6 us
    dot_general x1, matrix products, local_step(): lax.dot_general(grad_last, w_down[LAYERS - 1], (((1,), (1,)), ((), ())),...  13 us
    dot_general x1, matrix products, local_step(): pre_act = jnp.dot(x_last, w_up[LAYERS - 1], preferred_element_type=F32)  10.9 us
    pallas_call x1, Pallas kernels, last_product(): pl.pallas_call(down_kernel, out_shape=jax.ShapeDtypeStruct((tokens, WIDTH...  10.5 us
  transfers between devices with their start and end apart: 4, of which 0 were waited for; matrix products, arithmetic and copies ran while one was open for 6% of the time, Pallas kernels for 3%

profile of v5, /device:TPU:0, one launch (start us, length us, event | category | flops | bytes accessed | tf_op | source)
XLA Modules:
  0.0 462.9 jit_solution(13584745283632718006)
XLA Ops:
  0.6 0.1 collective-permute-start.1
  0.7 2.6 slice_bitcast_fusion
  3.3 0.0 copy-start.1
  3.3 0.0 copy-start
  3.3 0.5 collective-permute-start
  3.8 10.9 %multiply_convert_fusion = (bf16[384,5120]{1,0:T(8,128)(2,1)}, f32[384,5120]{1,0:T(8,128)S(1)}) fusion(bf16[2,1280,5120]{2,1,0:T(8,128)(2,1)} %w_up.1, bf16[2,1,384,1280]{3,2,1,0:T(8,128)(2,1)} %param.13), kind=kOutput, calls=%fused_computation.15 | convolution fusion | flops 5050859520 | bytes 25886720 | tf_op jit(solution)/shard_map/dot_general | solution.py:970
  14.7 0.0 copy-done.1
  14.7 0.2 collective-permute-start.3
  14.9 0.0 copy-done
  14.9 13.0 %fusion.12.right.d_last = bf16[384,5120]{1,0:T(8,128)(2,1)} fusion(f32[384,5120]{1,0:T(8,128)S(1)} %get-tuple-element.50, bf16[2,5120,1280]{2,1,0:T(8,128)(2,1)} %w_down.1, bf16[1,384,1280]{2,1,0:T(8,128)(2,1)S(1)} %copy-done), kind=kOutput, calls=%fused_computation.14 | convolution fusion | flops 5072486400 | bytes 25886720 | tf_op jit(solution)/shard_map/dot_general | solution.py:973
  27.9 0.0 collective-permute-done.1.right_pair
  27.9 0.0 copy-start.3
  27.9 0.0 collective-permute-done.left_pair
  27.9 0.0 copy-start.2
  28.0 1.0 copy-done.2
  29.0 0.3 collective-permute-start.2
  29.3 0.0 copy-done.3
  29.3 0.0 collective-permute-done.3.left_pair
  29.3 14.0 %grad_down.1.refs_0_ = f32[16,4,2,80,640]{4,3,2,1,0:T(8,128)} custom-call(s32[1]{0:T(128)} %bitcast.core_ref, bf16[384,5120]{1,0:T(8,128)(2,1)} %get-tuple-element.49.left, bf16[384,5120]{1,0:T(8,128)(2,1)} %collective-permute-done.3.left_pair, bf16[384,1280]{1,0:T(8,128)(2,1)} %bitcast.35, bf16[384,1280]{1,0:T(8,128)(2,1)} %copy-done.3), custom_call_target="tpu_custom_call" | custom-call | flops 5033164800 | bytes 17000000 | tf_op jit(solution)/shard_map/grad_down/pallas_call | solution.py:712
  43.2 0.0 collective-permute-done.2.right_pair
  43.2 12.6 %grad_up.1 = f32[16,4,2,80,640]{4,3,2,1,0:T(8,128)} custom-call(s32[1]{0:T(128)} %bitcast.core_ref, bf16[384,1280]{1,0:T(8,128)(2,1)} %copy-done.1, bf16[384,1280]{1,0:T(8,128)(2,1)} %copy-done.2, bf16[384,5120]{1,0:T(8,128)(2,1)} %fusion.12.right.d_last, bf16[384,5120]{1,0:T(8,128)(2,1)} %collective-permute-done.2.right_pair, ...), custom_call_target="tpu_custom_call", output_to_operand_aliasing={{}: (5, {})} | custom-call | flops 5033164800 | bytes 17000000 | tf_op jit(solution)/shard_map/grad_up/pallas_call | solution.py:712
  55.8 240.8 %torus_reduce.1 = (f32[320,640]{1,0:T(8,128)}, f32[4,4,4,160,640]{4,3,2,1,0:T(8,128)}, bf16[384,1280]{1,0:T(8,128)(2,1)}, bf16[384,2560]{1,0:T(8,128)(2,1)}, bf1...) custom-call(f32[4,4,4,160,640]{4,3,2,1,0:T(8,128)} %bitcast.32, ...), custom_call_target="tpu_custom_call" | custom-call | tf_op jit(solution)/shard_map/torus_reduce/pallas_call | solution.py:480
  296.7 29.6 %update_rows.1 = (bf16[320,640]{1,0:T(8,128)(2,1)}, f32[10,2,5120]{2,1,0:T(2,128)}, f32[2,40,1280]{2,1,0:T(8,128)}, f32[10,2,5120]{2,1,0:T(2,128)}, f32[2,40,128...) custom-call(f32[320,640]{1,0:T(8,128)} %get-tuple-element.30.block, f32[10,2,5120]{2,1,0:T(2,128)} %bitcast.39, ...), custom_call_target="tpu_custom_call" | custom-call | tf_op jit(solution)/shard_map/update_rows/pallas_call | solution.py:921
  326.3 123.1 %torus_gather_forward.1 = (bf16[2,4,4,4,320,640]{5,4,3,2,1,0:T(8,128)(2,1)}, bf16[384,1280]{1,0:T(8,128)(2,1)}, bf16[384,5120]{1,0:T(8,128)(2,1)}) custom-call(bf16[320,640]{1,0:T(8,128)(2,1)} %get-tuple-element.31.block_ref, bf16[384,1280]{1,0:T(8,128)(2,1)} %bitcast.38), custom_call_target="tpu_custom_call" | custom-call | tf_op jit(solution)/shard_map/torus_gather_forward/pallas_call | solution.py:669
  449.4 10.5 %forward_down.1 = bf16[384,1280]{1,0:T(8,128)(2,1)} custom-call(bf16[384,5120]{1,0:T(8,128)(2,1)} %get-tuple-element.32.act, bf16[2,16,4,4,80,640]{5,4,3,2,1,0:T(8,128)(2,1)} %bitcast.33, bf16[384,1280]{1,0:T(8,128)(2,1)} %get-tuple-element.34.hidden), custom_call_target="tpu_custom_call" | custom-call | tf_op jit(solution)/shard_map/forward_down/pallas_call | solution.py:749
  459.8 3.1 keep.1
Async XLA Ops:
  0.6 27.3 %collective-permute-start.1 = (bf16[384,1280]{1,0:T(8,128)(2,1)}, bf16[384,1280]{1,0:T(8,128)(2,1)S(1)}, u32[]{:S(2)}, u32[]{:S(2)}) collective-permute-start(bf16[384,1280]{1,0:T(8,128)(2,1)} %bitcast.34), channel_id=1, source_target_pairs={{0,1},{1,0},{2,3},{3,2},{4,5},{5,4},{6,7},{7,6},{8,9},{9,8},{10,11... | collective-permute-start | bytes 2949128 | tf_op jit(solution)/shard_map/ppermute | solution.py:958
  3.3 11.4 %copy-start.1 = (bf16[384,1280]{1,0:T(8,128)(2,1)}, bf16[384,1280]{1,0:T(8,128)(2,1)S(1)}, u32[]{:S(2)}) copy-start(bf16[384,1280]{1,0:T(8,128)(2,1)S(1)} %get-tuple-element.48.left) | copy-start | bytes 2949124
  3.3 11.6 %copy-start = (bf16[1,384,1280]{2,1,0:T(8,128)(2,1)S(1)}, bf16[1,384,1280]{2,1,0:T(8,128)(2,1)}, u32[]{:S(2)}) copy-start(bf16[1,384,1280]{2,1,0:T(8,128)(2,1)} %param.14) | copy-start | bytes 2949124
  3.3 24.6 %collective-permute-start = (bf16[384,1280]{1,0:T(8,128)(2,1)S(1)}, bf16[384,1280]{1,0:T(8,128)(2,1)S(1)}, u32[]{:S(2)}, u32[]{:S(2)}) collective-permute-start(bf16[384,1280]{1,0:T(8,128)(2,1)S(1)} %get-tuple-element.48.left), channel_id=1, source_target_pairs={{0,1},{1,0},{2,3},{3,2},{4,5},{5,4},{6,7},{7,6},{8,9},{9,8},{10,11... | collective-permute-start | bytes 2949128 | tf_op jit(solution)/shard_map/ppermute | solution.py:958
  14.7 14.6 %collective-permute-start.3 = (bf16[384,5120]{1,0:T(8,128)(2,1)}, bf16[384,5120]{1,0:T(8,128)(2,1)}, u32[]{:S(2)}, u32[]{:S(2)}) collective-permute-start(bf16[384,5120]{1,0:T(8,128)(2,1)} %get-tuple-element.49.left), channel_id=1, source_target_pairs={{0,1},{1,0},{2,3},{3,2},{4,5},{5,4},{6,7},{7,6},{8,9},{9,8},{10,11... | collective-permute-start | bytes 11796488 | tf_op jit(solution)/shard_map/ppermute | solution.py:958
  27.9 1.3 copy-start.3
  27.9 1.0 copy-start.2
  29.0 14.3 %collective-permute-start.2 = (bf16[384,5120]{1,0:T(8,128)(2,1)}, bf16[384,5120]{1,0:T(8,128)(2,1)}, u32[]{:S(2)}, u32[]{:S(2)}) collective-permute-start(bf16[384,5120]{1,0:T(8,128)(2,1)} %fusion.12.right.d_last), channel_id=1, source_target_pairs={{0,1},{1,0},{2,3},{3,2},{4,5},{5,4},{6,7},{7,6},{8,9},{9,8},{10,11... | collective-permute-start | bytes 11796488 | tf_op jit(solution)/shard_map/ppermute | solution.py:958

commit v6 on v5

--- a/solution.py
+++ b/solution.py
@@ -430,17 +430,26 @@
                 copy(0, 0, f, step, BATCH_START[0][f] + k, None).wait_send()
         pl.semaphore_signal(credit.at[f], inc=1, device_id=(source[f],), device_id_type=MESH)
 
-    @pl.loop(0, STEPS * TICKS)
+    done = STEPS * TICKS - SUM_TICK
+    ticks_left = (TILES - done) // 2
+
+    @pl.loop(0, ticks_left)
     def _(n):
         tick(1, 0, n)
-        job = n + STEPS * TICKS - SUM_TICK
-        pl.when(job < TILES)(functools.partial(compute, job))
+
+        @pl.loop(0, 2)
+        def _(i):
+            compute(done + 2 * n + i)
 
     for slot in range(2):
         tile_write(UP_TILES + slot, False).wait()
     for f in FLOWS:
         pl.semaphore_wait(credit.at[f], 1)
     start_batch(1)
+
+    @pl.loop(ticks_left, STEPS * TICKS)
+    def _(n):
+        tick(1, 0, n)
 
     @pl.loop(0, STEPS * TICKS)
     def _(n):

time: 464 us -> 470 us (1.013)
  Pallas kernels: 434 us -> 440 us
    pallas_call x1, Pallas kernels: 241 us -> 247 us  [reduce_blocks(): pl.pallas_call(reduce_kernel, out_shape=[jax.ShapeDtypeStruct((ROWS, COLS...]
where the time goes in v6:
time: 470 us; the launch traced here: 469 us
  Pallas kernels  440 us (94%)
  matrix products  23.9 us (5%)
    pallas_call x1, Pallas kernels, reduce_blocks(): pl.pallas_call(reduce_kernel, out_shape=[jax.ShapeDtypeStruct((ROWS, COLS...  247 us
    pallas_call x1, Pallas kernels, gather_forward(): pl.pallas_call(gather_kernel, out_shape=[jax.ShapeDtypeStruct((2, RING, R...  123 us
    pallas_call x1, Pallas kernels, update_rows(): pl.pallas_call(update_kernel, out_shape=[jax.ShapeDtypeStruct((ROWS, COLS...  29.6 us
    pallas_call x2, Pallas kernels, grad_sum(): pl.pallas_call(grad_kernel, out_shape=jax.ShapeDtypeStruct((zy, RING, 2,...  26.6 us
    dot_general x1, matrix products, local_step(): lax.dot_general(grad_last, w_down[LAYERS - 1], (((1,), (1,)), ((), ())),...  13 us
    dot_general x1, matrix products, local_step(): pre_act = jnp.dot(x_last, w_up[LAYERS - 1], preferred_element_type=F32)  10.9 us
    pallas_call x1, Pallas kernels, last_product(): pl.pallas_call(down_kernel, out_shape=jax.ShapeDtypeStruct((tokens, WIDTH...  10.5 us
  transfers between devices with their start and end apart: 4, of which 0 were waited for; matrix products, arithmetic and copies ran while one was open for 6% of the time, Pallas kernels for 3%

profile of v6, /device:TPU:0, one launch (start us, length us, event | category | flops | bytes accessed | tf_op | source)
XLA Modules:
  0.0 469.0 jit_solution(7971155577203075722)
XLA Ops:
  0.6 0.1 collective-permute-start.1
  0.7 2.6 slice_bitcast_fusion
  3.3 0.0 copy-start.1
  3.3 0.0 copy-start
  3.3 0.5 collective-permute-start
  3.8 10.9 %multiply_convert_fusion = (bf16[384,5120]{1,0:T(8,128)(2,1)}, f32[384,5120]{1,0:T(8,128)S(1)}) fusion(bf16[2,1280,5120]{2,1,0:T(8,128)(2,1)} %w_up.1, bf16[2,1,384,1280]{3,2,1,0:T(8,128)(2,1)} %param.13), kind=kOutput, calls=%fused_computation.15 | convolution fusion | flops 5050859520 | bytes 25886720 | tf_op jit(solution)/shard_map/dot_general | solution.py:979
  14.7 0.0 copy-done.1
  14.7 0.2 collective-permute-start.3
  14.9 0.0 copy-done
  14.9 13.0 %fusion.12.right.d_last = bf16[384,5120]{1,0:T(8,128)(2,1)} fusion(f32[384,5120]{1,0:T(8,128)S(1)} %get-tuple-element.50, bf16[2,5120,1280]{2,1,0:T(8,128)(2,1)} %w_down.1, bf16[1,384,1280]{2,1,0:T(8,128)(2,1)S(1)} %copy-done), kind=kOutput, calls=%fused_computation.14 | convolution fusion | flops 5072486400 | bytes 25886720 | tf_op jit(solution)/shard_map/dot_general | solution.py:982
  27.9 0.0 collective-permute-done.1.right_pair
  27.9 0.0 copy-start.3
  27.9 0.0 collective-permute-done.left_pair
  27.9 0.0 copy-start.2
  28.0 1.0 copy-done.2
  29.0 0.3 collective-permute-start.2
  29.3 0.0 copy-done.3
  29.3 0.0 collective-permute-done.3.left_pair
  29.3 14.0 %grad_down.1.refs_0_ = f32[16,4,2,80,640]{4,3,2,1,0:T(8,128)} custom-call(s32[1]{0:T(128)} %bitcast.core_ref, bf16[384,5120]{1,0:T(8,128)(2,1)} %get-tuple-element.49.left, bf16[384,5120]{1,0:T(8,128)(2,1)} %collective-permute-done.3.left_pair, bf16[384,1280]{1,0:T(8,128)(2,1)} %bitcast.35, bf16[384,1280]{1,0:T(8,128)(2,1)} %copy-done.3), custom_call_target="tpu_custom_call" | custom-call | flops 5033164800 | bytes 17000000 | tf_op jit(solution)/shard_map/grad_down/pallas_call | solution.py:721
  43.2 0.0 collective-permute-done.2.right_pair
  43.2 12.6 %grad_up.1 = f32[16,4,2,80,640]{4,3,2,1,0:T(8,128)} custom-call(s32[1]{0:T(128)} %bitcast.core_ref, bf16[384,1280]{1,0:T(8,128)(2,1)} %copy-done.1, bf16[384,1280]{1,0:T(8,128)(2,1)} %copy-done.2, bf16[384,5120]{1,0:T(8,128)(2,1)} %fusion.12.right.d_last, bf16[384,5120]{1,0:T(8,128)(2,1)} %collective-permute-done.2.right_pair, ...), custom_call_target="tpu_custom_call", output_to_operand_aliasing={{}: (5, {})} | custom-call | flops 5033164800 | bytes 17000000 | tf_op jit(solution)/shard_map/grad_up/pallas_call | solution.py:721
  55.8 246.9 %torus_reduce.1 = (f32[320,640]{1,0:T(8,128)}, f32[4,4,4,160,640]{4,3,2,1,0:T(8,128)}, bf16[384,1280]{1,0:T(8,128)(2,1)}, bf16[384,2560]{1,0:T(8,128)(2,1)}, bf1...) custom-call(f32[4,4,4,160,640]{4,3,2,1,0:T(8,128)} %bitcast.32, ...), custom_call_target="tpu_custom_call" | custom-call | tf_op jit(solution)/shard_map/torus_reduce/pallas_call | solution.py:489
  302.8 29.6 %update_rows.1 = (bf16[320,640]{1,0:T(8,128)(2,1)}, f32[10,2,5120]{2,1,0:T(2,128)}, f32[2,40,1280]{2,1,0:T(8,128)}, f32[10,2,5120]{2,1,0:T(2,128)}, f32[2,40,128...) custom-call(f32[320,640]{1,0:T(8,128)} %get-tuple-element.30.block, f32[10,2,5120]{2,1,0:T(2,128)} %bitcast.39, ...), custom_call_target="tpu_custom_call" | custom-call | tf_op jit(solution)/shard_map/update_rows/pallas_call | solution.py:930
  332.4 123.1 %torus_gather_forward.1 = (bf16[2,4,4,4,320,640]{5,4,3,2,1,0:T(8,128)(2,1)}, bf16[384,1280]{1,0:T(8,128)(2,1)}, bf16[384,5120]{1,0:T(8,128)(2,1)}) custom-call(bf16[320,640]{1,0:T(8,128)(2,1)} %get-tuple-element.31.block_ref, bf16[384,1280]{1,0:T(8,128)(2,1)} %bitcast.38), custom_call_target="tpu_custom_call" | custom-call | tf_op jit(solution)/shard_map/torus_gather_forward/pallas_call | solution.py:678
  455.5 10.5 %forward_down.1 = bf16[384,1280]{1,0:T(8,128)(2,1)} custom-call(bf16[384,5120]{1,0:T(8,128)(2,1)} %get-tuple-element.32.act, bf16[2,16,4,4,80,640]{5,4,3,2,1,0:T(8,128)(2,1)} %bitcast.33, bf16[384,1280]{1,0:T(8,128)(2,1)} %get-tuple-element.34.hidden), custom_call_target="tpu_custom_call" | custom-call | tf_op jit(solution)/shard_map/forward_down/pallas_call | solution.py:758
  466.0 3.1 keep.1
Async XLA Ops:
  0.6 27.3 %collective-permute-start.1 = (bf16[384,1280]{1,0:T(8,128)(2,1)}, bf16[384,1280]{1,0:T(8,128)(2,1)S(1)}, u32[]{:S(2)}, u32[]{:S(2)}) collective-permute-start(bf16[384,1280]{1,0:T(8,128)(2,1)} %bitcast.34), channel_id=1, source_target_pairs={{0,1},{1,0},{2,3},{3,2},{4,5},{5,4},{6,7},{7,6},{8,9},{9,8},{10,11... | collective-permute-start | bytes 2949128 | tf_op jit(solution)/shard_map/ppermute | solution.py:967
  3.3 11.4 %copy-start.1 = (bf16[384,1280]{1,0:T(8,128)(2,1)}, bf16[384,1280]{1,0:T(8,128)(2,1)S(1)}, u32[]{:S(2)}) copy-start(bf16[384,1280]{1,0:T(8,128)(2,1)S(1)} %get-tuple-element.48.left) | copy-start | bytes 2949124
  3.3 11.6 %copy-start = (bf16[1,384,1280]{2,1,0:T(8,128)(2,1)S(1)}, bf16[1,384,1280]{2,1,0:T(8,128)(2,1)}, u32[]{:S(2)}) copy-start(bf16[1,384,1280]{2,1,0:T(8,128)(2,1)} %param.14) | copy-start | bytes 2949124
  3.3 24.6 %collective-permute-start = (bf16[384,1280]{1,0:T(8,128)(2,1)S(1)}, bf16[384,1280]{1,0:T(8,128)(2,1)S(1)}, u32[]{:S(2)}, u32[]{:S(2)}) collective-permute-start(bf16[384,1280]{1,0:T(8,128)(2,1)S(1)} %get-tuple-element.48.left), channel_id=1, source_target_pairs={{0,1},{1,0},{2,3},{3,2},{4,5},{5,4},{6,7},{7,6},{8,9},{9,8},{10,11... | collective-permute-start | bytes 2949128 | tf_op jit(solution)/shard_map/ppermute | solution.py:967
  14.7 14.6 %collective-permute-start.3 = (bf16[384,5120]{1,0:T(8,128)(2,1)}, bf16[384,5120]{1,0:T(8,128)(2,1)}, u32[]{:S(2)}, u32[]{:S(2)}) collective-permute-start(bf16[384,5120]{1,0:T(8,128)(2,1)} %get-tuple-element.49.left), channel_id=1, source_target_pairs={{0,1},{1,0},{2,3},{3,2},{4,5},{5,4},{6,7},{7,6},{8,9},{9,8},{10,11... | collective-permute-start | bytes 11796488 | tf_op jit(solution)/shard_map/ppermute | solution.py:967
  27.9 1.3 copy-start.3
  27.9 1.0 copy-start.2
  29.0 14.3 %collective-permute-start.2 = (bf16[384,5120]{1,0:T(8,128)(2,1)}, bf16[384,5120]{1,0:T(8,128)(2,1)}, u32[]{:S(2)}, u32[]{:S(2)}) collective-permute-start(bf16[384,5120]{1,0:T(8,128)(2,1)} %fusion.12.right.d_last), channel_id=1, source_target_pairs={{0,1},{1,0},{2,3},{3,2},{4,5},{5,4},{6,7},{7,6},{8,9},{9,8},{10,11... | collective-permute-start | bytes 11796488 | tf_op jit(solution)/shard_map/ppermute | solution.py:967
